TPU v7x, 512 devices: a 8x2x16 block of a 8x8x16 slice. The times are simulated.
512 devices in a mesh: blocks: 2 (over y), gz: 128 (over z, x), gy: 2 (over core).
Axes of the slice: x: 8, y: 2, z: 16, core: 2. Of those that a mesh axis runs over, the one named last changes fastest.
The devices are a block of a 8x8x16 slice.
Arguments:
- view_a: float32 [4096, 32, 512], P(('blocks', 'gz'), 'gy'), parts along dimension 0, may hold values from 0.5 to 2
- view_b_own: float32 [1024, 32, 2048], P(('blocks', 'gz'), 'gy'), parts along dimension 0, may hold values from 0.5 to 2
- spread_a: float32 [3, 31], replicated, may hold values from 0.05 to 1
- spread_b: float32 [3, 31], replicated, may hold values from 0.05 to 1
Outputs:
- estimate: float32 [4096, 32, 512], P(('blocks', 'gz'), 'gy'), parts along dimension 0
There are 2 independent parts, one for each index of `blocks`. A program takes and returns all parts, laid end to end along the dimension named above; an argument that names none is the same for every part. Nothing has to cross between parts.
All inputs are finite; a program needn't handle non-finite values.
Results may differ from a plain program's by a relative error of at most 0.0001.
Values sent between devices are 32-bit elements; how exact they have to be, the bound alone decides.
No kernel may reach another device: no remote copies, remote signals or barrier semaphores. Data moves between devices by JAX's collectives and lax.ppermute only.
A program may use at most 64 MiB of HBM per device.

v0:
```python
import jax
import jax.numpy as jnp
from jax import lax
from jax.sharding import PartitionSpec as P


def padded(cells, sides, width):
    for axis, dim in sides:
        count = lax.axis_size(axis)
        ends = count - 1
        head = lax.slice_in_dim(cells, 0, width, axis=dim)
        tail = lax.slice_in_dim(cells, cells.shape[dim] - width, cells.shape[dim], axis=dim)
        cells = jnp.concatenate(
            [
                lax.ppermute(tail, axis, [(i, (i + 1) % count) for i in range(ends)]),
                cells,
                lax.ppermute(head, axis, [((i + 1) % count, i) for i in range(ends)]),
            ],
            axis=dim,
        )
    return cells


def band_table(weights, count_in, count_out, offset):
    source = jnp.arange(count_in, dtype=jnp.int32)[:, None]
    target = jnp.arange(count_out, dtype=jnp.int32)[None, :]
    spread = source - target + offset
    table = jnp.zeros((count_in, count_out), jnp.float32)
    for place in range(weights.shape[0]):
        table = table + jnp.where(spread == place, weights[place], jnp.float32(0.0))
    return table


def blur(volume, kernels):
    count_z, count_y, count_x = volume.shape
    radius = (kernels.shape[1] - 1) // 2
    table_x = band_table(kernels[2], count_x, count_x, radius)
    along_x = jnp.einsum("zyx,xw->zyw", volume, table_x, precision=lax.Precision.HIGHEST)
    table_y = band_table(kernels[1], count_y + 2 * radius, count_y, 0)
    widened = padded(along_x, (("gy", 1),), radius)
    narrow_y = jnp.einsum("zyx,yw->zwx", widened, table_y, precision=lax.Precision.HIGHEST)
    along_y = padded(narrow_y, (("gz", 0),), radius)
    table_z = band_table(kernels[0], count_z + 2 * radius, count_z, 0)
    return jnp.einsum("zyx,zw->wyx", along_y, table_z, precision=lax.Precision.HIGHEST)


def shards(view_a, view_b_own, spread_a, spread_b):
    arrived = lax.all_to_all(view_b_own, "gz", split_axis=2, concat_axis=0, tiled=True)
    view_b = jnp.transpose(arrived, (2, 1, 0))[:, :, ::-1]
    blur_a = spread_a / jnp.sum(spread_a, axis=1, keepdims=True)
    blur_b = spread_b / jnp.sum(spread_b, axis=1, keepdims=True)
    estimate = 0.5 * (view_a + view_b)
    for measured, kernels in ((view_a, blur_a), (view_b, blur_b)):
        quotient = measured / blur(estimate, kernels)
        estimate = estimate * blur(quotient, kernels[:, ::-1])
    return estimate


def solution(mesh):
    in_specs = (P(("blocks", "gz"), "gy", None), P(("blocks", "gz"), "gy", None), P(), P())
    out_specs = P(("blocks", "gz"), "gy", None)
    return jax.shard_map(shards, mesh=mesh, in_specs=in_specs, out_specs=out_specs, check_vma=False)
```

profile of v0, /device:TPU:192, one launch (start us, length us, event | category | flops | bytes accessed | tf_op | source)
XLA Modules:
  0.0 484.0 jit_solution(18353538417334878022)
XLA Ops:
  0.0 4.4 copy.22
  4.5 5.4 %reshape.758 = f32[128,1,1024]{2,1,0:T(1,128)} reshape(f32[2048,4,16]{2,1,0:T(4,128)} %bitcast.238) | data formatting | bytes 1048576
  9.9 50.9 %all-to-all-start = ((f32[128,1,1024]{2,1,0:T(1,128)}), f32[128,1,1024]{2,1,0:T(1,128)S(1)}, u32[]{:S(2)}, u32[]{:S(2)}) async-start(f32[128,1,1024]{2,1,0:T(1,128)} %reshape.758), calls=%async_computation | async-start | bytes 1048576 | tf_op jit(solution)/shard_map/all_to_all | solution.py:48
  61.0 0.7 fusion.2087
  61.7 0.7 fusion.2088
  62.5 31.2 %all-to-all-done = f32[128,1,1024]{2,1,0:T(1,128)S(1)} async-done(((f32[128,1,1024]{2,1,0:T(1,128)}), f32[128,1,1024]{2,1,0:T(1,128)S(1)}, u32[]{:S(2)}, u32[]{:S(2)}) %all-to-all-start) | async-done | bytes 524320 | tf_op jit(solution)/shard_map/all_to_all | solution.py:48
  93.7 0.5 broadcast.2035
  94.2 1.9 reduce
  96.1 4.2 reshape.759
  100.3 5.3 %copy.38 = f32[4,16,128,16]{3,1,0,2:T(8,128)} copy(f32[4,16,128,16]{1,0,3,2:T(4,128)} %bitcast.239) | data formatting | bytes 1048576 | tf_op jit(solution)/shard_map/all_to_all | solution.py:48
  105.7 2.8 copy.25
  108.5 0.5 rev.2
  109.1 0.4 add_multiply_fusion
  109.4 25.2 %fusion.122 = f32[16,16,512]{2,1,0:T(8,128)S(1)} fusion(f32[16,16,512]{2,0,1:T(8,128)S(1)} %add_multiply_fusion, f32[]{:T(128)} %bitcast.101, f32[]{:T(128)} %bitcast.100, f32[]{:T(128)} %bitcast.99, f32[]{:T(128)} %bitcast.98, f32[]{:T(128)} %bitcast.97, f32[]{:T(128)} %bitcast.96, f32[]{:T(128)} %bitcast.95, f32[]{:T(128)} %bitcast.94, f32[]{:T(128)} %bitcast.93, ...), kind=kOutput, calls=%fused_computation.114 | convolution fusion | flops 829947904 | bytes 1048700 | tf_op jit(solution)/shard_map/zyx,xw->zyw/dot_general | solution.py:38
  134.8 1.3 collective-permute-start.1
  136.1 3.1 collective-permute-start
  139.2 0.7 fusion.2089
  140.0 0.7 fusion.2090
  140.7 20.5 %fusion.53 = f32[16,16,512]{2,1,0:T(8,128)S(1)} fusion(f32[16,15,512]{2,1,0:T(8,128)S(1)} %collective-permute-done.1, f32[16,16,512]{2,1,0:T(8,128)S(1)} %fusion.122, f32[16,15,512]{2,1,0:T(8,128)S(1)} %collective-permute-done, f32[]{:T(128)} %bitcast.67, f32[]{:T(128)} %bitcast.66, f32[]{:T(128)} %bitcast.65, f32[]{:T(128)} %bitcast.64, f32[]{:T(128)} %bitcast.63, ...), kind=kOutput, calls=%fused_computation.47 | convolution fusion | flops 73173856 | bytes 2031740 | tf_op jit(solution)/shard_map/zyx,yw->zwx/dot_general | solution.py:41
  161.4 4.8 collective-permute-start.3
  166.2 2.1 collective-permute-start.2
  168.3 0.7 fusion.2091
  169.1 8.2 %collective-permute-done.3 = f32[15,16,512]{2,1,0:T(8,128)S(1)} collective-permute-done((f32[15,16,512]{2,1,0:T(8,128)S(1)}, f32[15,16,512]{2,1,0:T(8,128)S(1)}, u32[]{:S(2)}, u32[]{:S(2)}) %collective-permute-start.3) | collective-permute-done | bytes 491552 | tf_op jit(solution)/shard_map/ppermute | solution.py:17
  177.2 6.3 %collective-permute-done.2 = f32[15,16,512]{2,1,0:T(8,128)S(1)} collective-permute-done((f32[15,16,512]{2,1,0:T(8,128)S(1)}, f32[15,16,512]{2,1,0:T(8,128)S(1)}, u32[]{:S(2)}, u32[]{:S(2)}) %collective-permute-start.2) | collective-permute-done | bytes 491552 | tf_op jit(solution)/shard_map/ppermute | solution.py:15
  183.5 0.2 pad_maximum_fusion
  183.7 20.9 %fusion.32 = f32[16,16,512]{2,0,1:T(8,128)S(1)} fusion(f32[46,16,512]{2,1,0:T(8,128)S(1)} %pad_maximum_fusion, f32[16,16,512]{2,1,0:T(8,128)S(1)} %copy-done, f32[]{:T(128)} %bitcast.35, f32[]{:T(128)} %bitcast.34, f32[]{:T(128)} %bitcast.33, f32[]{:T(128)} %bitcast.32, f32[]{:T(128)} %bitcast.31, f32[]{:T(128)} %bitcast.30, f32[]{:T(128)} %bitcast.29, ...), kind=kOutput, calls=%fused_computation.40 | convolution fusion | flops 72551264 | bytes 2556028 | tf_op jit(solution)/shard_map/zyx,zw->wyx/dot_general | solution.py:44
  204.6 25.2 %fusion.120 = f32[16,16,512]{2,1,0:T(8,128)S(1)} fusion(f32[16,16,512]{2,0,1:T(8,128)S(1)} %fusion.32, f32[]{:T(128)} %bitcast.101, f32[]{:T(128)} %bitcast.100, f32[]{:T(128)} %bitcast.99, f32[]{:T(128)} %bitcast.98, f32[]{:T(128)} %bitcast.97, f32[]{:T(128)} %bitcast.96, f32[]{:T(128)} %bitcast.95, f32[]{:T(128)} %bitcast.94, f32[]{:T(128)} %bitcast.93, ...), kind=kOutput, calls=%fused_computation.112 | convolution fusion | flops 829947904 | bytes 1048700 | tf_op jit(solution)/shard_map/zyx,xw->zyw/dot_general | solution.py:38
  229.9 1.3 collective-permute-start.5
  231.3 3.1 collective-permute-start.4
  234.4 1.5 collective-permute-done.4
  235.9 20.5 %fusion.50 = f32[16,16,512]{2,1,0:T(8,128)S(1)} fusion(f32[16,15,512]{2,1,0:T(8,128)S(1)} %collective-permute-done.5, f32[16,16,512]{2,1,0:T(8,128)S(1)} %fusion.120, f32[16,15,512]{2,1,0:T(8,128)S(1)} %collective-permute-done.4, f32[]{:T(128)} %bitcast.67, f32[]{:T(128)} %bitcast.66, f32[]{:T(128)} %bitcast.65, f32[]{:T(128)} %bitcast.64, f32[]{:T(128)} %bitcast.63, ...), kind=kOutput, calls=%fused_computation.46 | convolution fusion | flops 73173856 | bytes 2031740 | tf_op jit(solution)/shard_map/zyx,yw->zwx/dot_general | solution.py:41
  256.4 0.9 fusion.2078
  257.3 1.9 collective-permute-start.7
  259.3 4.2 collective-permute-start.6
  263.7 0.7 fusion.2082
  264.4 0.7 fusion.2083
  265.1 7.8 %collective-permute-done.7 = f32[15,16,512]{2,1,0:T(8,128)S(1)} collective-permute-done((f32[15,16,512]{2,1,0:T(8,128)}, f32[15,16,512]{2,1,0:T(8,128)S(1)}, u32[]{:S(2)}, u32[]{:S(2)}) %collective-permute-start.7) | collective-permute-done | bytes 491552 | tf_op jit(solution)/shard_map/ppermute | solution.py:17
  273.0 3.9 collective-permute-done.6
  277.0 20.7 %fusion.35 = f32[16,16,512]{2,0,1:T(8,128)S(1)} fusion(f32[16,16,512]{2,0,1:T(8,128)S(1)} %add_multiply_fusion, f32[46,16,512]{2,1,0:T(8,128)S(1)} %pad_maximum_fusion.1, f32[]{:T(128)} %bitcast.35, f32[]{:T(128)} %bitcast.34, f32[]{:T(128)} %bitcast.33, f32[]{:T(128)} %bitcast.32, f32[]{:T(128)} %bitcast.31, f32[]{:T(128)} %bitcast.30, f32[]{:T(128)} %bitcast.29, ...), kind=kOutput, calls=%fused_computation.41 | convolution fusion | flops 72551264 | bytes 2556028 | tf_op jit(solution)/shard_map/zyx,zw->wyx/dot_general | solution.py:44
  297.7 25.4 %fusion.118 = f32[16,16,512]{2,1,0:T(8,128)S(1)} fusion(f32[16,16,512]{2,0,1:T(8,128)S(1)} %fusion.35, f32[]{:T(128)} %bitcast.202, f32[]{:T(128)} %bitcast.201, f32[]{:T(128)} %bitcast.200, f32[]{:T(128)} %bitcast.199, f32[]{:T(128)} %bitcast.198, f32[]{:T(128)} %bitcast.197, f32[]{:T(128)} %bitcast.196, f32[]{:T(128)} %bitcast.195, f32[]{:T(128)} %bitcast.194, ...), kind=kOutput, calls=%fused_computation.110 | convolution fusion | flops 829947904 | bytes 1048700 | tf_op jit(solution)/shard_map/zyx,xw->zyw/dot_general | solution.py:38
  323.2 1.3 collective-permute-start.9
  324.5 3.1 collective-permute-start.8
  327.7 0.7 fusion.2084
  328.4 0.7 fusion.2085
  329.2 20.2 %fusion.47 = f32[16,16,512]{2,1,0:T(8,128)S(1)} fusion(f32[16,15,512]{2,1,0:T(8,128)S(1)} %collective-permute-done.9, f32[16,16,512]{2,1,0:T(8,128)S(1)} %fusion.118, f32[16,15,512]{2,1,0:T(8,128)S(1)} %collective-permute-done.8, f32[]{:T(128)} %bitcast.168, f32[]{:T(128)} %bitcast.167, f32[]{:T(128)} %bitcast.166, f32[]{:T(128)} %bitcast.165, ...), kind=kOutput, calls=%fused_computation.45 | convolution fusion | flops 73173856 | bytes 2031740 | tf_op jit(solution)/shard_map/zyx,yw->zwx/dot_general | solution.py:41
  349.5 2.0 collective-permute-start.11
  351.5 4.2 collective-permute-start.10
  355.7 0.7 fusion.2086
  356.4 8.5 %collective-permute-done.11 = f32[15,16,512]{2,1,0:T(8,128)S(1)} collective-permute-done((f32[15,16,512]{2,1,0:T(8,128)S(1)}, f32[15,16,512]{2,1,0:T(8,128)S(1)}, u32[]{:S(2)}, u32[]{:S(2)}) %collective-permute-start.11) | collective-permute-done | bytes 491552 | tf_op jit(solution)/shard_map/ppermute | solution.py:17
  364.9 4.1 collective-permute-done.10
  369.0 0.2 pad_maximum_fusion.2
  369.2 20.9 %fusion.38 = f32[16,16,512]{2,0,1:T(8,128)S(1)} fusion(f32[16,16,512]{2,0,1:T(8,128)S(1)} %rev.2, f32[46,16,512]{2,1,0:T(8,128)S(1)} %pad_maximum_fusion.2, f32[]{:T(128)} %bitcast.136, f32[]{:T(128)} %bitcast.135, f32[]{:T(128)} %bitcast.134, f32[]{:T(128)} %bitcast.133, f32[]{:T(128)} %bitcast.132, f32[]{:T(128)} %bitcast.131, f32[]{:T(128)} %bitcast.130, ...), kind=kOutput, calls=%fused_computation.42 | convolution fusion | flops 72551264 | bytes 2556028 | tf_op jit(solution)/shard_map/zyx,zw->wyx/dot_general | solution.py:44
  390.1 25.4 %fusion.116 = f32[16,16,512]{2,1,0:T(8,128)S(1)} fusion(f32[16,16,512]{2,0,1:T(8,128)S(1)} %fusion.38, f32[]{:T(128)} %bitcast.202, f32[]{:T(128)} %bitcast.201, f32[]{:T(128)} %bitcast.200, f32[]{:T(128)} %bitcast.199, f32[]{:T(128)} %bitcast.198, f32[]{:T(128)} %bitcast.197, f32[]{:T(128)} %bitcast.196, f32[]{:T(128)} %bitcast.195, f32[]{:T(128)} %bitcast.194, ...), kind=kOutput, calls=%fused_computation.108 | convolution fusion | flops 829947904 | bytes 1048700 | tf_op jit(solution)/shard_map/zyx,xw->zyw/dot_general | solution.py:38
  415.7 1.3 collective-permute-start.13
  417.0 3.1 collective-permute-start.12
  420.2 1.5 collective-permute-done.12
  421.6 20.2 %fusion.44 = f32[16,16,512]{2,1,0:T(8,128)S(1)} fusion(f32[16,15,512]{2,1,0:T(8,128)S(1)} %collective-permute-done.13, f32[16,16,512]{2,1,0:T(8,128)S(1)} %fusion.116, f32[16,15,512]{2,1,0:T(8,128)S(1)} %collective-permute-done.12, f32[]{:T(128)} %bitcast.168, f32[]{:T(128)} %bitcast.167, f32[]{:T(128)} %bitcast.166, f32[]{:T(128)} %bitcast.165, ...), kind=kOutput, calls=%fused_computation.44 | convolution fusion | flops 73173856 | bytes 2031740 | tf_op jit(solution)/shard_map/zyx,yw->zwx/dot_general | solution.py:41
  442.0 2.0 collective-permute-start.15
  444.0 4.0 collective-permute-start.14
  447.9 9.5 %collective-permute-done.15 = f32[15,16,512]{2,1,0:T(8,128)S(1)} collective-permute-done((f32[15,16,512]{2,1,0:T(8,128)S(1)}, f32[15,16,512]{2,1,0:T(8,128)S(1)}, u32[]{:S(2)}, u32[]{:S(2)}) %collective-permute-start.15) | collective-permute-done | bytes 491552 | tf_op jit(solution)/shard_map/ppermute | solution.py:17
  457.4 4.1 collective-permute-done.14
  461.5 0.2 pad_maximum_fusion.3
  461.7 20.9 %fusion.41 = f32[16,16,512]{2,0,1:T(8,128)S(1)} fusion(f32[16,16,512]{2,0,1:T(8,128)S(1)} %fusion.35, f32[46,16,512]{2,1,0:T(8,128)S(1)} %pad_maximum_fusion.3, f32[]{:T(128)} %bitcast.136, f32[]{:T(128)} %bitcast.135, f32[]{:T(128)} %bitcast.134, f32[]{:T(128)} %bitcast.133, f32[]{:T(128)} %bitcast.132, f32[]{:T(128)} %bitcast.131, f32[]{:T(128)} %bitcast.130, ...), kind=kOutput, calls=%fused_computation.43 | convolution fusion | flops 72551264 | bytes 2556028 | tf_op jit(solution)/shard_map/zyx,zw->wyx/dot_general | solution.py:44
  482.6 1.1 copy.36
  (24 shorter events, 1.3 us)
Async XLA Ops:
  4.4 56.3 %copy-start.1 = (f32[3,31]{1,0:T(4,128)S(1)}, f32[3,31]{1,0:T(4,128)}, u32[]{:S(2)}) copy-start(f32[3,31]{1,0:T(4,128)} %param.6) | copy-start | bytes 1120
  9.9 83.8 %all-to-all-start = ((f32[128,1,1024]{2,1,0:T(1,128)}), f32[128,1,1024]{2,1,0:T(1,128)S(1)}, u32[]{:S(2)}, u32[]{:S(2)}) async-start(f32[128,1,1024]{2,1,0:T(1,128)} %reshape.758), calls=%async_computation | async-start | bytes 1048576 | tf_op jit(solution)/shard_map/all_to_all | solution.py:48
  105.7 3.4 copy-start
  134.8 5.9 %collective-permute-start.1 = (f32[16,15,512]{2,1,0:T(8,128)S(1)}, f32[16,15,512]{2,1,0:T(8,128)S(1)}, u32[]{:S(2)}, u32[]{:S(2)}) collective-permute-start(f32[16,15,512]{2,1,0:T(8,128)S(1)} %get-tuple-element.20), channel_id=1, source_target_pairs={{1,0},{3,2},{5,4},{7,6},{9,8},{11,10},{13,12},{15,14},{17,16},{19,... | collective-permute-start | bytes 1474568 | tf_op jit(solution)/shard_map/ppermute | solution.py:17
  136.1 4.6 collective-permute-start
  161.4 15.8 %collective-permute-start.3 = (f32[15,16,512]{2,1,0:T(8,128)S(1)}, f32[15,16,512]{2,1,0:T(8,128)S(1)}, u32[]{:S(2)}, u32[]{:S(2)}) collective-permute-start(f32[15,16,512]{2,1,0:T(8,128)S(1)} %get-tuple-element.18), channel_id=1, source_target_pairs={{2,0},{4,2},{6,4},{8,6},{10,8},{12,10},{14,12},{16,14},{18,16},{20... | collective-permute-start | bytes 1474568 | tf_op jit(solution)/shard_map/ppermute | solution.py:17
  166.2 17.3 %collective-permute-start.2 = (f32[15,16,512]{2,1,0:T(8,128)S(1)}, f32[15,16,512]{2,1,0:T(8,128)S(1)}, u32[]{:S(2)}, u32[]{:S(2)}) collective-permute-start(f32[15,16,512]{2,1,0:T(8,128)S(1)} %get-tuple-element.17), channel_id=1, source_target_pairs={{0,2},{2,4},{4,6},{6,8},{8,10},{10,12},{12,14},{14,16},{16,18},{18... | collective-permute-start | bytes 1474568 | tf_op jit(solution)/shard_map/ppermute | solution.py:15
  229.9 4.5 collective-permute-start.5
  231.2 32.2 %copy-start.2 = (f32[3,31]{1,0:T(4,128)S(1)}, f32[3,31]{1,0:T(4,128)}, u32[]{:S(2)}) copy-start(f32[3,31]{1,0:T(4,128)} %param.7) | copy-start | bytes 1120
  231.3 4.6 collective-permute-start.4
  257.3 15.6 %collective-permute-start.7 = (f32[15,16,512]{2,1,0:T(8,128)}, f32[15,16,512]{2,1,0:T(8,128)S(1)}, u32[]{:S(2)}, u32[]{:S(2)}) collective-permute-start(f32[15,16,512]{2,1,0:T(8,128)} %get-tuple-element.14), channel_id=1, source_target_pairs={{2,0},{4,2},{6,4},{8,6},{10,8},{12,10},{14,12},{16,14},{18,16},{20... | collective-permute-start | bytes 1474568 | tf_op jit(solution)/shard_map/ppermute | solution.py:17
  259.3 17.5 %collective-permute-start.6 = (f32[15,16,512]{2,1,0:T(8,128)S(1)}, f32[15,16,512]{2,1,0:T(8,128)S(1)}, u32[]{:S(2)}, u32[]{:S(2)}) collective-permute-start(f32[15,16,512]{2,1,0:T(8,128)S(1)} %get-tuple-element.13), channel_id=1, source_target_pairs={{0,2},{2,4},{4,6},{6,8},{8,10},{10,12},{12,14},{14,16},{16,18},{18... | collective-permute-start | bytes 1474568 | tf_op jit(solution)/shard_map/ppermute | solution.py:15
  323.2 5.9 %collective-permute-start.9 = (f32[16,15,512]{2,1,0:T(8,128)S(1)}, f32[16,15,512]{2,1,0:T(8,128)S(1)}, u32[]{:S(2)}, u32[]{:S(2)}) collective-permute-start(f32[16,15,512]{2,1,0:T(8,128)S(1)} %get-tuple-element.12), channel_id=1, source_target_pairs={{1,0},{3,2},{5,4},{7,6},{9,8},{11,10},{13,12},{15,14},{17,16},{19,... | collective-permute-start | bytes 1474568 | tf_op jit(solution)/shard_map/ppermute | solution.py:17
  324.5 4.6 collective-permute-start.8
  349.5 15.4 %collective-permute-start.11 = (f32[15,16,512]{2,1,0:T(8,128)S(1)}, f32[15,16,512]{2,1,0:T(8,128)S(1)}, u32[]{:S(2)}, u32[]{:S(2)}) collective-permute-start(f32[15,16,512]{2,1,0:T(8,128)S(1)} %get-tuple-element.10), channel_id=1, source_target_pairs={{2,0},{4,2},{6,4},{8,6},{10,8},{12,10},{14,12},{16,14},{18,16},{20... | collective-permute-start | bytes 1474568 | tf_op jit(solution)/shard_map/ppermute | solution.py:17
  351.5 17.5 %collective-permute-start.10 = (f32[15,16,512]{2,1,0:T(8,128)S(1)}, f32[15,16,512]{2,1,0:T(8,128)S(1)}, u32[]{:S(2)}, u32[]{:S(2)}) collective-permute-start(f32[15,16,512]{2,1,0:T(8,128)S(1)} %get-tuple-element.9), channel_id=1, source_target_pairs={{0,2},{2,4},{4,6},{6,8},{8,10},{10,12},{12,14},{14,16},{16,18},{18... | collective-permute-start | bytes 1474568 | tf_op jit(solution)/shard_map/ppermute | solution.py:15
  415.7 4.5 collective-permute-start.13
  417.0 4.6 collective-permute-start.12
  442.0 15.4 %collective-permute-start.15 = (f32[15,16,512]{2,1,0:T(8,128)S(1)}, f32[15,16,512]{2,1,0:T(8,128)S(1)}, u32[]{:S(2)}, u32[]{:S(2)}) collective-permute-start(f32[15,16,512]{2,1,0:T(8,128)S(1)} %get-tuple-element.6), channel_id=1, source_target_pairs={{2,0},{4,2},{6,4},{8,6},{10,8},{12,10},{14,12},{16,14},{18,16},{20... | collective-permute-start | bytes 1474568 | tf_op jit(solution)/shard_map/ppermute | solution.py:17
  444.0 17.5 %collective-permute-start.14 = (f32[15,16,512]{2,1,0:T(8,128)S(1)}, f32[15,16,512]{2,1,0:T(8,128)S(1)}, u32[]{:S(2)}, u32[]{:S(2)}) collective-permute-start(f32[15,16,512]{2,1,0:T(8,128)S(1)} %get-tuple-element.5), channel_id=1, source_target_pairs={{0,2},{2,4},{4,6},{6,8},{8,10},{10,12},{12,14},{14,16},{16,18},{18... | collective-permute-start | bytes 1474568 | tf_op jit(solution)/shard_map/ppermute | solution.py:15
where the time goes:
time: 492 us; the launch traced here: 484 us
  matrix products  266 us (54%)
  starting transfers between devices  93.8 us (19%)
  waiting for transfers between devices  86.6 us (18%)
  local copies, waits for them, and re-layouts  33.3 us (7%)
    dot_general x4, matrix products, blur(): jnp.einsum('zyx,xw->zyw', volume, table_x, precision=lax.Precision.HIGHEST)  101 us
    dot_general x4, matrix products, blur(): jnp.einsum('zyx,zw->wyx', along_y, table_z, precision=lax.Precision.HIGHEST)  83.5 us
    dot_general x4, matrix products, blur(): jnp.einsum('zyx,yw->zwx', widened, table_y, precision=lax.Precision.HIGHEST)  81.6 us
    all_to_all x1, starting transfers between devices, shards(): lax.all_to_all(view_b_own, 'gz', split_axis=2, concat_axis=0, tiled=True)  50.9 us
    ppermute x8, waiting for transfers between devices, padded(): lax.ppermute(head, axis, [((i + 1) % count, i) for i in range(ends)])  34 us
    all_to_all x1, waiting for transfers between devices, shards(): lax.all_to_all(view_b_own, 'gz', split_axis=2, concat_axis=0, tiled=True)  31.2 us
    ppermute x8, starting transfers between devices, padded(): lax.ppermute(tail, axis, [(i, (i + 1) % count) for i in range(ends)])  27 us
    ppermute x8, waiting for transfers between devices, padded(): lax.ppermute(tail, axis, [(i, (i + 1) % count) for i in range(ends)])  21.3 us
  transfers between devices with their start and end apart: 17, of which 11 were waited for; matrix products, arithmetic and copies ran while one was open for 2% of the time, Pallas kernels for 0%

commit v1 on v0

v1 whole, which is shorter than its diff:
```python
import functools

import jax
import jax.numpy as jnp
from jax import lax
from jax.experimental import pallas as pl
from jax.experimental.pallas import tpu as pltpu
from jax.sharding import PartitionSpec as P

BF16 = jnp.bfloat16
F32 = jnp.float32
MIB = 1 << 20


def halves(values):
    high = values.astype(BF16)
    low = (values - high.astype(F32)).astype(BF16)
    return high, low


def product(left, right):
    dot = functools.partial(jnp.dot, preferred_element_type=F32)
    return dot(left[0], right[0]) + (dot(left[0], right[1]) + dot(left[1], right[0]))


def pick(weights, axis, place, shape):
    spread, flipped = weights
    taps = spread.shape[1]
    table = jnp.zeros(shape, F32)
    total = jnp.zeros(shape[-2:], F32)[:1, :1]
    for tap in range(taps):
        value = spread[axis, taps - 1 - tap if flipped else tap]
        table = jnp.where(place == tap, value, table)
        total = total + value
    return table / total


def put(high_ref, low_ref, where, values):
    high, low = halves(values)
    high_ref[where] = high
    low_ref[where] = low


def tables_kernel(planes, rows, flipped, spread_ref, core, xh, xl, yh, yl, oh, ol, zh, zl, lh, ll, rh, rl):
    weights = (spread_ref, flipped)
    radius = spread_ref.shape[1] // 2
    count_x = xh.shape[0]
    lane = 128
    spread = lax.broadcasted_iota(jnp.int32, (lane, lane), 0) - lax.broadcasted_iota(jnp.int32, (lane, lane), 1)
    blocks = {
        shift: halves(pick(weights, 2, spread + (radius + shift * lane), (lane, lane)))
        for shift in (-1, 0, 1)
    }
    nothing = jnp.zeros((lane, lane), BF16)
    for row in range(count_x // lane):
        for column in range(count_x // lane):
            where = (slice(row * lane, (row + 1) * lane), slice(column * lane, (column + 1) * lane))
            high, low = blocks.get(row - column, (nothing, nothing))
            xh[where] = high
            xl[where] = low
    cells = planes * rows
    edge = radius * rows
    target = lax.broadcasted_iota(jnp.int32, (rows, cells), 0)
    column = lax.broadcasted_iota(jnp.int32, (rows, cells), 1)
    source, plane = column % rows, column // rows
    near = pick(weights, 1, source - target + radius, (rows, cells))
    side = rows * (1 - 2 * core[0])
    far = pick(weights, 1, source - target + radius + side, (rows, cells))
    same = source == target
    edge_same, edge_plane = same[:, :edge], plane[:, :edge]

    def one_plane(at, carry):
        where = (pl.ds(pl.multiple_of(at * rows, rows), rows), slice(None))
        zero = jnp.zeros((), F32)
        put(yh, yl, where, jnp.where(plane == at, near, zero))
        put(oh, ol, where, jnp.where(plane == at, far, zero))
        middle = pick(weights, 0, plane - at + radius, (rows, cells))
        put(zh, zl, where, jnp.where(same, middle, zero))
        left = pick(weights, 0, edge_plane - at, (rows, edge))
        put(lh, ll, where, jnp.where(edge_same, left, zero))
        right = pick(weights, 0, edge_plane - at + (planes + radius), (rows, edge))
        put(rh, rl, where, jnp.where(edge_same, right, zero))
        return carry

    lax.fori_loop(0, planes, one_plane, 0)


def vmem(count):
    return [pl.BlockSpec(memory_space=pltpu.VMEM)] * count


def params(mib):
    return pltpu.CompilerParams(vmem_limit_bytes=mib * MIB)


def cost(flops, moved):
    return pl.CostEstimate(flops=flops, bytes_accessed=moved, transcendentals=0)


def tables(spread, flipped, core, planes, rows, count_x):
    radius = spread.shape[1] // 2
    cells, edge = planes * rows, radius * rows
    shapes = [(count_x, count_x), (cells, cells), (cells, cells), (cells, cells), (cells, edge), (cells, edge)]
    out = [jax.ShapeDtypeStruct(shape, BF16) for shape in shapes for _ in range(2)]
    return pl.pallas_call(
        functools.partial(tables_kernel, planes, rows, flipped),
        out_shape=out,
        in_specs=[pl.BlockSpec(memory_space=pltpu.SMEM)] * 2,
        out_specs=vmem(len(out)),
        compiler_params=params(6),
        cost_estimate=cost(10**7, 4 * 10**6),
        name="tables",
    )(spread, core)


def pack_kernel(planes, own, messages):
    lane = 128
    half = planes // 2
    for block in range(own.shape[1] // lane):
        turned = own[:, block * lane:(block + 1) * lane].T
        for slab in range(lane // planes):
            at = slab * planes
            tile = jnp.concatenate([turned[at:at + half], turned[at + half:at + planes]], axis=1)
            to = block * (lane // planes) + slab
            messages[to * half:(to + 1) * half, :] = tile


def pack(own, planes):
    per_slab, rows, count_z = own.shape
    return pl.pallas_call(
        functools.partial(pack_kernel, planes),
        out_shape=jax.ShapeDtypeStruct((count_z // 2, 2 * per_slab * rows), F32),
        in_specs=vmem(1),
        out_specs=vmem(1)[0],
        compiler_params=params(4),
        cost_estimate=cost(10**6, 10**6),
        name="pack",
    )(own.reshape(per_slab * rows, count_z))


def order_kernel(per_slab, order):
    count_x = order.shape[0]
    slabs = count_x // per_slab
    source = lax.broadcasted_iota(jnp.int32, order.shape, 0)
    target = lax.broadcasted_iota(jnp.int32, order.shape, 1)
    wanted = count_x - 1 - (per_slab * (source % slabs) + source // slabs)
    order[...] = jnp.where(target == wanted, F32(1.0), F32(0.0)).astype(BF16)


def ordering(count_x, per_slab):
    return pl.pallas_call(
        functools.partial(order_kernel, per_slab),
        out_shape=jax.ShapeDtypeStruct((count_x, count_x), BF16),
        out_specs=vmem(1)[0],
        compiler_params=params(4),
        cost_estimate=cost(10**6, 10**6),
        name="ordering",
    )()


def start_kernel(planes, per_slab, messages, view, order, xh, xl, second, estimate, along_x, gathered):
    half = planes // 2
    rows = view.shape[0] // planes
    slabs = messages.shape[0] // half
    for z in range(half):
        turned = messages[pl.ds(z, slabs, stride=half), :].T
        for part in range(2):
            for x in range(per_slab):
                at = (part * per_slab + x) * rows
                to = (part * half + z) * rows
                gathered[to:to + rows, x * slabs:(x + 1) * slabs] = turned[at:at + rows]
    values = gathered[...]
    high = values.astype(BF16)
    rest = values - high.astype(F32)
    middle = rest.astype(BF16)
    low = (rest - middle.astype(F32)).astype(BF16)
    dot = functools.partial(jnp.dot, preferred_element_type=F32)
    moved = (dot(high, order[...]) + dot(middle, order[...])) + dot(low, order[...])
    second[...] = moved
    first = 0.5 * (view[...] + moved)
    estimate[...] = first
    along_x[...] = product(halves(first), (xh[...], xl[...]))


def start(messages, view, order, table, planes):
    cells, count_x = view.shape
    per_slab = count_x * planes // 2 // messages.shape[0]
    block = jax.ShapeDtypeStruct(view.shape, F32)
    return pl.pallas_call(
        functools.partial(start_kernel, planes, per_slab),
        out_shape=[block] * 3,
        in_specs=vmem(5),
        out_specs=vmem(3),
        scratch_shapes=[pltpu.VMEM(view.shape, F32)],
        compiler_params=params(6),
        cost_estimate=cost(10**9, 3 * 10**6),
        name="start",
    )(messages, view, order, *table[0:2])


def across_y_kernel(edge, own, other, yh, yl, oh, ol, whole, head, tail):
    result = product((yh[...], yl[...]), halves(own[...])) + product((oh[...], ol[...]), halves(other[...]))
    whole[...] = result
    head[...] = result[:edge]
    tail[...] = result[result.shape[0] - edge:]


def across_y(own, other, table, edge):
    whole = jax.ShapeDtypeStruct(own.shape, F32)
    piece = jax.ShapeDtypeStruct((edge, own.shape[1]), F32)
    return pl.pallas_call(
        functools.partial(across_y_kernel, edge),
        out_shape=[whole, piece, piece],
        in_specs=vmem(6),
        out_specs=vmem(3),
        compiler_params=params(6),
        cost_estimate=cost(10**9, 3 * 10**6),
        name="across_y",
    )(own, other, *table[2:6])


def across_z_kernel(kind, left, own, right, zh, zl, lh, ll, rh, rl, factor, *rest):
    blurred = product((zh[...], zl[...]), halves(own[...])) + (
        product((lh[...], ll[...]), halves(left[...])) + product((rh[...], rl[...]), halves(right[...]))
    )
    if kind == "last":
        rest[0][...] = factor[...] * blurred
        return
    if kind == "quotient":
        xh, xl, along_x = rest
        value = factor[...] / blurred
    else:
        xh, xl, updated, along_x = rest
        value = factor[...] * blurred
        updated[...] = value
    along_x[...] = product(halves(value), (xh[...], xl[...]))


def across_z(kind, left, own, right, table, factor, following):
    operands = [left, own, right, *table[6:12], factor]
    if kind != "last":
        operands += following[0:2]
    block = jax.ShapeDtypeStruct(own.shape, F32)
    count = 2 if kind == "update" else 1
    return pl.pallas_call(
        functools.partial(across_z_kernel, kind),
        out_shape=[block] * count,
        in_specs=vmem(len(operands)),
        out_specs=vmem(count),
        compiler_params=params(6),
        cost_estimate=cost(10**9, 4 * 10**6),
        name="across_z_" + kind,
    )(*operands)


def shards(view_a, view_b_own, spread_a, spread_b):
    planes, rows, count_x = view_a.shape
    cells = planes * rows
    radius = spread_a.shape[1] // 2
    edge = radius * rows
    slabs = lax.axis_size("gz")
    per_slab = view_b_own.shape[0]
    first = view_a.reshape(cells, count_x)

    packed = pack(view_b_own, planes)
    lanes = packed.shape[1]
    arrived = lax.all_to_all(packed.reshape(slabs, -1, lanes), "gz", 0, 0, tiled=True)
    arrived = arrived.reshape(-1, lanes)

    core = lax.axis_index("gy").astype(jnp.int32).reshape(1)
    steps = [
        tables(spread, flipped, core, planes, rows, count_x)
        for spread in (spread_a, spread_b)
        for flipped in (False, True)
    ]
    order = ordering(count_x, per_slab)

    swap = [(0, 1), (1, 0)]
    up = [(i, i + 1) for i in range(slabs - 1)]
    down = [(i + 1, i) for i in range(slabs - 1)]

    second, estimate, along_x = start(arrived, first, order, steps[0], planes)
    for step, table in enumerate(steps):
        other = lax.ppermute(along_x, "gy", swap)
        whole, head, tail = across_y(along_x, other, table, edge)
        left = lax.ppermute(tail, "gz", up)
        right = lax.ppermute(head, "gz", down)
        if step % 2 == 0:
            measured = first if step == 0 else second
            (along_x,) = across_z("quotient", left, whole, right, table, measured, steps[step + 1])
        elif step + 1 < len(steps):
            estimate, along_x = across_z("update", left, whole, right, table, estimate, steps[step + 1])
        else:
            (estimate,) = across_z("last", left, whole, right, table, estimate, None)
    return estimate.reshape(planes, rows, count_x)


def solution(mesh):
    in_specs = (P(("blocks", "gz"), "gy", None), P(("blocks", "gz"), "gy", None), P(), P())
    out_specs = P(("blocks", "gz"), "gy", None)
    return jax.shard_map(shards, mesh=mesh, in_specs=in_specs, out_specs=out_specs, check_vma=False)
```

time: 492 us -> 190 us (0.39)
  the two profiles are of different devices: /device:TPU:192 before, /device:TPU:94 now
where the time goes in v1:
time: 190 us
  waiting for transfers between devices  83.8 us (44%)
  starting transfers between devices  83 us (44%)
  Pallas kernels  19.2 us (10%)
  local copies, waits for them, and re-layouts  3.59 us (2%)
    all_to_all x1, starting transfers between devices, shards(): lax.all_to_all(packed.reshape(slabs, -1, lanes), 'gz', 0, 0, tiled=True)  51.4 us
    ppermute x4, waiting for transfers between devices, shards(): left = lax.ppermute(tail, 'gz', up)  30.4 us
    all_to_all x1, waiting for transfers between devices, shards(): lax.all_to_all(packed.reshape(slabs, -1, lanes), 'gz', 0, 0, tiled=True)  28.7 us
    ppermute x4, waiting for transfers between devices, shards(): right = lax.ppermute(head, 'gz', down)  17.2 us
    ppermute x4, starting transfers between devices, shards(): right = lax.ppermute(head, 'gz', down)  14.8 us
    ppermute x4, starting transfers between devices, shards(): left = lax.ppermute(tail, 'gz', up)  9.01 us
    pallas_call x4, Pallas kernels, tables(): pl.pallas_call(functools.partial(tables_kernel, planes, rows, flipped), o...  8.62 us
    ppermute x4, starting transfers between devices, shards(): other = lax.ppermute(along_x, 'gy', swap)  7.8 us
  transfers between devices with their start and end apart: 13, of which 13 were waited for; matrix products, arithmetic and copies ran while one was open for 0% of the time, Pallas kernels for 5%

profile of v1, /device:TPU:94, one launch (start us, length us, event | category | flops | bytes accessed | tf_op | source)
XLA Modules:
  0.0 189.9 jit_solution(9637967725375322921)
XLA Ops:
  0.0 0.0 copy-start.1
  0.0 1.0 copy-done.1
  1.0 1.3 pack.1
  2.3 51.4 %all-to-all-start = ((f32[128,8,128]{2,1,0:T(8,128)}), f32[128,8,128]{2,1,0:T(8,128)S(1)}, u32[]{:S(2)}, u32[]{:S(2)}) async-start(f32[128,8,128]{2,1,0:T(8,128)} %bitcast.1), calls=%async_computation | async-start | bytes 1048576 | tf_op jit(solution)/shard_map/all_to_all | solution.py:267
  53.8 0.0 copy-start
  53.8 0.0 copy-start.2
  53.8 0.1 ordering.1.order
  53.9 0.6 copy-done.2
  54.5 2.2 %tables.4 = (bf16[512,512]{1,0:T(8,128)(2,1)S(1)}, bf16[512,512]{1,0:T(8,128)(2,1)S(1)}, bf16[256,256]{1,0:T(8,128)(2,1)S(1)}, bf16[256,256]{1,0:T(8,128)(2,1)S(...) custom-call(f32[3,31]{1,0:T(4,128)S(1)} %copy-done.2, ...), custom_call_target="tpu_custom_call" | custom-call | flops 10000000 | bytes 4000000 | tf_op jit(solution)/shard_map/tables/pallas_call | solution.py:105
  56.7 0.0 copy-start.4
  56.7 0.6 copy-done.4
  57.3 0.0 copy-start.6
  57.3 0.6 copy-done.6
  58.0 0.0 copy-start.8
  58.0 0.6 copy-done.8
  58.6 28.7 %all-to-all-done = f32[128,8,128]{2,1,0:T(8,128)S(1)} async-done(((f32[128,8,128]{2,1,0:T(8,128)}), f32[128,8,128]{2,1,0:T(8,128)S(1)}, u32[]{:S(2)}, u32[]{:S(2)}) %all-to-all-start) | async-done | bytes 524320 | tf_op jit(solution)/shard_map/all_to_all | solution.py:267
  87.4 0.0 copy-done
  87.4 0.0 copy-start.5
  87.4 0.0 copy-start.7
  87.4 0.0 copy-start.9
  87.4 1.3 start.1
  88.6 2.0 %collective-permute-start = (f32[256,512]{1,0:T(8,128)S(1)}, f32[256,512]{1,0:T(8,128)S(1)}, u32[]{:S(2)}, u32[]{:S(2)}) collective-permute-start(f32[256,512]{1,0:T(8,128)S(1)} %get-tuple-element.72.own), channel_id=1, source_target_pairs={{0,1},{1,0},{2,3},{3,2},{4,5},{5,4},{6,7},{7,6},{8,9},{9,8},{10,11... | collective-permute-start | bytes 1572872 | tf_op jit(solution)/shard_map/ppermute | solution.py:284
  90.6 1.9 collective-permute-done.other
  92.5 0.0 copy-done.5
  92.5 0.0 copy-done.7
  92.5 0.0 copy-done.9
  92.5 0.6 across_y.4
  93.1 3.2 %collective-permute-start.1 = (f32[240,512]{1,0:T(8,128)S(1)}, f32[240,512]{1,0:T(8,128)S(1)}, u32[]{:S(2)}, u32[]{:S(2)}) collective-permute-start(f32[240,512]{1,0:T(8,128)S(1)} %get-tuple-element.77), channel_id=1, source_target_pairs={{0,2},{2,4},{4,6},{6,8},{8,10},{10,12},{12,14},{14,16},{16,18},{18... | collective-permute-start | bytes 1474568 | tf_op jit(solution)/shard_map/ppermute | solution.py:286
  96.3 2.7 %collective-permute-start.2 = (f32[240,512]{1,0:T(8,128)S(1)}, f32[240,512]{1,0:T(8,128)S(1)}, u32[]{:S(2)}, u32[]{:S(2)}) collective-permute-start(f32[240,512]{1,0:T(8,128)S(1)} %get-tuple-element.79), channel_id=1, source_target_pairs={{2,0},{4,2},{6,4},{8,6},{10,8},{12,10},{14,12},{16,14},{18,16},{20... | collective-permute-start | bytes 1474568 | tf_op jit(solution)/shard_map/ppermute | solution.py:287
  99.0 2.2 %tables.5 = (bf16[512,512]{1,0:T(8,128)(2,1)S(1)}, bf16[512,512]{1,0:T(8,128)(2,1)S(1)}, bf16[256,256]{1,0:T(8,128)(2,1)S(1)}, bf16[256,256]{1,0:T(8,128)(2,1)S(...) custom-call(f32[3,31]{1,0:T(4,128)S(1)} %copy-done.2, ...), custom_call_target="tpu_custom_call" | custom-call | flops 10000000 | bytes 4000000 | tf_op jit(solution)/shard_map/tables/pallas_call | solution.py:105
  101.2 7.1 %collective-permute-done.1.left = f32[240,512]{1,0:T(8,128)S(1)} collective-permute-done((f32[240,512]{1,0:T(8,128)S(1)}, f32[240,512]{1,0:T(8,128)S(1)}, u32[]{:S(2)}, u32[]{:S(2)}) %collective-permute-start.1) | collective-permute-done | bytes 491552 | tf_op jit(solution)/shard_map/ppermute | solution.py:286
  108.3 5.0 %collective-permute-done.2.right = f32[240,512]{1,0:T(8,128)S(1)} collective-permute-done((f32[240,512]{1,0:T(8,128)S(1)}, f32[240,512]{1,0:T(8,128)S(1)}, u32[]{:S(2)}, u32[]{:S(2)}) %collective-permute-start.2) | collective-permute-done | bytes 491552 | tf_op jit(solution)/shard_map/ppermute | solution.py:287
  113.3 1.3 across_z_quotient.2.own
  114.6 2.0 %collective-permute-start.3 = (f32[256,512]{1,0:T(8,128)S(1)}, f32[256,512]{1,0:T(8,128)S(1)}, u32[]{:S(2)}, u32[]{:S(2)}) collective-permute-start(f32[256,512]{1,0:T(8,128)S(1)} %across_z_quotient.2.own), channel_id=1, source_target_pairs={{0,1},{1,0},{2,3},{3,2},{4,5},{5,4},{6,7},{7,6},{8,9},{9,8},{10,11... | collective-permute-start | bytes 1572872 | tf_op jit(solution)/shard_map/ppermute | solution.py:284
  116.5 1.9 collective-permute-done.3.other
  118.4 0.6 across_y.5
  119.0 0.0 copy-start.3
  119.1 2.0 %collective-permute-start.4 = (f32[240,512]{1,0:T(8,128)S(1)}, f32[240,512]{1,0:T(8,128)S(1)}, u32[]{:S(2)}, u32[]{:S(2)}) collective-permute-start(f32[240,512]{1,0:T(8,128)S(1)} %get-tuple-element.92), channel_id=1, source_target_pairs={{0,2},{2,4},{4,6},{6,8},{8,10},{10,12},{12,14},{14,16},{16,18},{18... | collective-permute-start | bytes 1474568 | tf_op jit(solution)/shard_map/ppermute | solution.py:286
  121.0 4.0 %collective-permute-start.5 = (f32[240,512]{1,0:T(8,128)S(1)}, f32[240,512]{1,0:T(8,128)S(1)}, u32[]{:S(2)}, u32[]{:S(2)}) collective-permute-start(f32[240,512]{1,0:T(8,128)S(1)} %get-tuple-element.94), channel_id=1, source_target_pairs={{2,0},{4,2},{6,4},{8,6},{10,8},{12,10},{14,12},{16,14},{18,16},{20... | collective-permute-start | bytes 1474568 | tf_op jit(solution)/shard_map/ppermute | solution.py:287
  125.0 0.0 copy-done.3
  125.0 2.2 %tables.6 = (bf16[512,512]{1,0:T(8,128)(2,1)S(1)}, bf16[512,512]{1,0:T(8,128)(2,1)S(1)}, bf16[256,256]{1,0:T(8,128)(2,1)S(1)}, bf16[256,256]{1,0:T(8,128)(2,1)S(...) custom-call(f32[3,31]{1,0:T(4,128)S(1)} %copy-done.3, ...), custom_call_target="tpu_custom_call" | custom-call | flops 10000000 | bytes 4000000 | tf_op jit(solution)/shard_map/tables/pallas_call | solution.py:105
  127.1 7.1 %collective-permute-done.4.left = f32[240,512]{1,0:T(8,128)S(1)} collective-permute-done((f32[240,512]{1,0:T(8,128)S(1)}, f32[240,512]{1,0:T(8,128)S(1)}, u32[]{:S(2)}, u32[]{:S(2)}) %collective-permute-start.4) | collective-permute-done | bytes 491552 | tf_op jit(solution)/shard_map/ppermute | solution.py:286
  134.2 4.1 %collective-permute-done.5.right = f32[240,512]{1,0:T(8,128)S(1)} collective-permute-done((f32[240,512]{1,0:T(8,128)S(1)}, f32[240,512]{1,0:T(8,128)S(1)}, u32[]{:S(2)}, u32[]{:S(2)}) %collective-permute-start.5) | collective-permute-done | bytes 491552 | tf_op jit(solution)/shard_map/ppermute | solution.py:287
  138.3 1.3 across_z_update.1
  139.6 2.0 %collective-permute-start.6 = (f32[256,512]{1,0:T(8,128)S(1)}, f32[256,512]{1,0:T(8,128)S(1)}, u32[]{:S(2)}, u32[]{:S(2)}) collective-permute-start(f32[256,512]{1,0:T(8,128)S(1)} %get-tuple-element.104.own), channel_id=1, source_target_pairs={{0,1},{1,0},{2,3},{3,2},{4,5},{5,4},{6,7},{7,6},{8,9},{9,8},{10,11... | collective-permute-start | bytes 1572872 | tf_op jit(solution)/shard_map/ppermute | solution.py:284
  141.6 1.9 collective-permute-done.6.other
  143.4 0.6 across_y.6
  144.1 2.0 %collective-permute-start.7 = (f32[240,512]{1,0:T(8,128)S(1)}, f32[240,512]{1,0:T(8,128)S(1)}, u32[]{:S(2)}, u32[]{:S(2)}) collective-permute-start(f32[240,512]{1,0:T(8,128)S(1)} %get-tuple-element.109), channel_id=1, source_target_pairs={{0,2},{2,4},{4,6},{6,8},{8,10},{10,12},{12,14},{14,16},{16,18},{18... | collective-permute-start | bytes 1474568 | tf_op jit(solution)/shard_map/ppermute | solution.py:286
  146.0 4.1 %collective-permute-start.8 = (f32[240,512]{1,0:T(8,128)S(1)}, f32[240,512]{1,0:T(8,128)S(1)}, u32[]{:S(2)}, u32[]{:S(2)}) collective-permute-start(f32[240,512]{1,0:T(8,128)S(1)} %get-tuple-element.111), channel_id=1, source_target_pairs={{2,0},{4,2},{6,4},{8,6},{10,8},{12,10},{14,12},{16,14},{18,16},{20... | collective-permute-start | bytes 1474568 | tf_op jit(solution)/shard_map/ppermute | solution.py:287
  150.2 2.2 %tables.7 = (bf16[512,512]{1,0:T(8,128)(2,1)S(1)}, bf16[512,512]{1,0:T(8,128)(2,1)S(1)}, bf16[256,256]{1,0:T(8,128)(2,1)S(1)}, bf16[256,256]{1,0:T(8,128)(2,1)S(...) custom-call(f32[3,31]{1,0:T(4,128)S(1)} %copy-done.3, ...), custom_call_target="tpu_custom_call" | custom-call | flops 10000000 | bytes 4000000 | tf_op jit(solution)/shard_map/tables/pallas_call | solution.py:105
  152.3 6.9 %collective-permute-done.7.left = f32[240,512]{1,0:T(8,128)S(1)} collective-permute-done((f32[240,512]{1,0:T(8,128)S(1)}, f32[240,512]{1,0:T(8,128)S(1)}, u32[]{:S(2)}, u32[]{:S(2)}) %collective-permute-start.7) | collective-permute-done | bytes 491552 | tf_op jit(solution)/shard_map/ppermute | solution.py:286
  159.3 4.1 %collective-permute-done.8.right = f32[240,512]{1,0:T(8,128)S(1)} collective-permute-done((f32[240,512]{1,0:T(8,128)S(1)}, f32[240,512]{1,0:T(8,128)S(1)}, u32[]{:S(2)}, u32[]{:S(2)}) %collective-permute-start.8) | collective-permute-done | bytes 491552 | tf_op jit(solution)/shard_map/ppermute | solution.py:287
  163.3 1.3 across_z_quotient.3.own
  164.6 2.0 %collective-permute-start.9 = (f32[256,512]{1,0:T(8,128)S(1)}, f32[256,512]{1,0:T(8,128)S(1)}, u32[]{:S(2)}, u32[]{:S(2)}) collective-permute-start(f32[256,512]{1,0:T(8,128)S(1)} %across_z_quotient.3.own), channel_id=1, source_target_pairs={{0,1},{1,0},{2,3},{3,2},{4,5},{5,4},{6,7},{7,6},{8,9},{9,8},{10,11... | collective-permute-start | bytes 1572872 | tf_op jit(solution)/shard_map/ppermute | solution.py:284
  166.6 1.9 collective-permute-done.9.other
  168.5 0.6 across_y.7
  169.1 2.0 %collective-permute-start.10 = (f32[240,512]{1,0:T(8,128)S(1)}, f32[240,512]{1,0:T(8,128)S(1)}, u32[]{:S(2)}, u32[]{:S(2)}) collective-permute-start(f32[240,512]{1,0:T(8,128)S(1)} %get-tuple-element.125), channel_id=1, source_target_pairs={{0,2},{2,4},{4,6},{6,8},{8,10},{10,12},{12,14},{14,16},{16,18},{18... | collective-permute-start | bytes 1474568 | tf_op jit(solution)/shard_map/ppermute | solution.py:286
  171.0 4.0 %collective-permute-start.11 = (f32[240,512]{1,0:T(8,128)S(1)}, f32[240,512]{1,0:T(8,128)S(1)}, u32[]{:S(2)}, u32[]{:S(2)}) collective-permute-start(f32[240,512]{1,0:T(8,128)S(1)} %get-tuple-element.127), channel_id=1, source_target_pairs={{2,0},{4,2},{6,4},{8,6},{10,8},{12,10},{14,12},{16,14},{18,16},{20... | collective-permute-start | bytes 1474568 | tf_op jit(solution)/shard_map/ppermute | solution.py:287
  175.0 9.3 %collective-permute-done.10.left = f32[240,512]{1,0:T(8,128)S(1)} collective-permute-done((f32[240,512]{1,0:T(8,128)S(1)}, f32[240,512]{1,0:T(8,128)S(1)}, u32[]{:S(2)}, u32[]{:S(2)}) %collective-permute-start.10) | collective-permute-done | bytes 491552 | tf_op jit(solution)/shard_map/ppermute | solution.py:286
  184.3 4.1 %collective-permute-done.11.right = f32[240,512]{1,0:T(8,128)S(1)} collective-permute-done((f32[240,512]{1,0:T(8,128)S(1)}, f32[240,512]{1,0:T(8,128)S(1)}, u32[]{:S(2)}, u32[]{:S(2)}) %collective-permute-start.11) | collective-permute-done | bytes 491552 | tf_op jit(solution)/shard_map/ppermute | solution.py:287
  188.3 1.6 across_z_last.1
Async XLA Ops:
  0.0 1.0 copy-start.1
  2.3 85.0 %all-to-all-start = ((f32[128,8,128]{2,1,0:T(8,128)}), f32[128,8,128]{2,1,0:T(8,128)S(1)}, u32[]{:S(2)}, u32[]{:S(2)}) async-start(f32[128,8,128]{2,1,0:T(8,128)} %bitcast.1), calls=%async_computation | async-start | bytes 1048576 | tf_op jit(solution)/shard_map/all_to_all | solution.py:267
  53.8 33.6 %copy-start = (f32[16,16,512]{2,1,0:T(8,128)S(1)}, f32[16,16,512]{2,1,0:T(8,128)}, u32[]{:S(2)}) copy-start(f32[16,16,512]{2,1,0:T(8,128)} %param.4) | copy-start | bytes 1572868
  53.8 0.7 copy-start.2
  56.7 0.7 copy-start.4
  57.3 0.6 copy-start.6
  58.0 0.7 copy-start.8
  87.4 5.1 %copy-start.5 = (bf16[256,256]{1,0:T(8,128)(2,1)S(1)}, bf16[256,256]{1,0:T(8,128)(2,1)}, u32[]{:S(2)}) copy-start(bf16[256,256]{1,0:T(8,128)(2,1)} %copy-done.4) | copy-start | bytes 393220
  87.4 5.1 %copy-start.7 = (bf16[256,256]{1,0:T(8,128)(2,1)S(1)}, bf16[256,256]{1,0:T(8,128)(2,1)}, u32[]{:S(2)}) copy-start(bf16[256,256]{1,0:T(8,128)(2,1)} %copy-done.6) | copy-start | bytes 393220
  87.4 5.1 %copy-start.9 = (bf16[256,256]{1,0:T(8,128)(2,1)S(1)}, bf16[256,256]{1,0:T(8,128)(2,1)}, u32[]{:S(2)}) copy-start(bf16[256,256]{1,0:T(8,128)(2,1)} %copy-done.8) | copy-start | bytes 393220
  88.6 3.8 %collective-permute-start = (f32[256,512]{1,0:T(8,128)S(1)}, f32[256,512]{1,0:T(8,128)S(1)}, u32[]{:S(2)}, u32[]{:S(2)}) collective-permute-start(f32[256,512]{1,0:T(8,128)S(1)} %get-tuple-element.72.own), channel_id=1, source_target_pairs={{0,1},{1,0},{2,3},{3,2},{4,5},{5,4},{6,7},{7,6},{8,9},{9,8},{10,11... | collective-permute-start | bytes 1572872 | tf_op jit(solution)/shard_map/ppermute | solution.py:284
  93.1 15.2 %collective-permute-start.1 = (f32[240,512]{1,0:T(8,128)S(1)}, f32[240,512]{1,0:T(8,128)S(1)}, u32[]{:S(2)}, u32[]{:S(2)}) collective-permute-start(f32[240,512]{1,0:T(8,128)S(1)} %get-tuple-element.77), channel_id=1, source_target_pairs={{0,2},{2,4},{4,6},{6,8},{8,10},{10,12},{12,14},{14,16},{16,18},{18... | collective-permute-start | bytes 1474568 | tf_op jit(solution)/shard_map/ppermute | solution.py:286
  96.3 17.0 %collective-permute-start.2 = (f32[240,512]{1,0:T(8,128)S(1)}, f32[240,512]{1,0:T(8,128)S(1)}, u32[]{:S(2)}, u32[]{:S(2)}) collective-permute-start(f32[240,512]{1,0:T(8,128)S(1)} %get-tuple-element.79), channel_id=1, source_target_pairs={{2,0},{4,2},{6,4},{8,6},{10,8},{12,10},{14,12},{16,14},{18,16},{20... | collective-permute-start | bytes 1474568 | tf_op jit(solution)/shard_map/ppermute | solution.py:287
  114.6 3.8 %collective-permute-start.3 = (f32[256,512]{1,0:T(8,128)S(1)}, f32[256,512]{1,0:T(8,128)S(1)}, u32[]{:S(2)}, u32[]{:S(2)}) collective-permute-start(f32[256,512]{1,0:T(8,128)S(1)} %across_z_quotient.2.own), channel_id=1, source_target_pairs={{0,1},{1,0},{2,3},{3,2},{4,5},{5,4},{6,7},{7,6},{8,9},{9,8},{10,11... | collective-permute-start | bytes 1572872 | tf_op jit(solution)/shard_map/ppermute | solution.py:284
  119.0 5.9 %copy-start.3 = (f32[3,31]{1,0:T(4,128)S(1)}, f32[3,31]{1,0:T(4,128)}, u32[]{:S(2)}) copy-start(f32[3,31]{1,0:T(4,128)} %spread_ref.7) | copy-start | bytes 1120
  119.1 15.2 %collective-permute-start.4 = (f32[240,512]{1,0:T(8,128)S(1)}, f32[240,512]{1,0:T(8,128)S(1)}, u32[]{:S(2)}, u32[]{:S(2)}) collective-permute-start(f32[240,512]{1,0:T(8,128)S(1)} %get-tuple-element.92), channel_id=1, source_target_pairs={{0,2},{2,4},{4,6},{6,8},{8,10},{10,12},{12,14},{14,16},{16,18},{18... | collective-permute-start | bytes 1474568 | tf_op jit(solution)/shard_map/ppermute | solution.py:286
  121.0 17.3 %collective-permute-start.5 = (f32[240,512]{1,0:T(8,128)S(1)}, f32[240,512]{1,0:T(8,128)S(1)}, u32[]{:S(2)}, u32[]{:S(2)}) collective-permute-start(f32[240,512]{1,0:T(8,128)S(1)} %get-tuple-element.94), channel_id=1, source_target_pairs={{2,0},{4,2},{6,4},{8,6},{10,8},{12,10},{14,12},{16,14},{18,16},{20... | collective-permute-start | bytes 1474568 | tf_op jit(solution)/shard_map/ppermute | solution.py:287
  139.6 3.8 %collective-permute-start.6 = (f32[256,512]{1,0:T(8,128)S(1)}, f32[256,512]{1,0:T(8,128)S(1)}, u32[]{:S(2)}, u32[]{:S(2)}) collective-permute-start(f32[256,512]{1,0:T(8,128)S(1)} %get-tuple-element.104.own), channel_id=1, source_target_pairs={{0,1},{1,0},{2,3},{3,2},{4,5},{5,4},{6,7},{7,6},{8,9},{9,8},{10,11... | collective-permute-start | bytes 1572872 | tf_op jit(solution)/shard_map/ppermute | solution.py:284
  144.1 15.2 %collective-permute-start.7 = (f32[240,512]{1,0:T(8,128)S(1)}, f32[240,512]{1,0:T(8,128)S(1)}, u32[]{:S(2)}, u32[]{:S(2)}) collective-permute-start(f32[240,512]{1,0:T(8,128)S(1)} %get-tuple-element.109), channel_id=1, source_target_pairs={{0,2},{2,4},{4,6},{6,8},{8,10},{10,12},{12,14},{14,16},{16,18},{18... | collective-permute-start | bytes 1474568 | tf_op jit(solution)/shard_map/ppermute | solution.py:286
  146.0 17.3 %collective-permute-start.8 = (f32[240,512]{1,0:T(8,128)S(1)}, f32[240,512]{1,0:T(8,128)S(1)}, u32[]{:S(2)}, u32[]{:S(2)}) collective-permute-start(f32[240,512]{1,0:T(8,128)S(1)} %get-tuple-element.111), channel_id=1, source_target_pairs={{2,0},{4,2},{6,4},{8,6},{10,8},{12,10},{14,12},{16,14},{18,16},{20... | collective-permute-start | bytes 1474568 | tf_op jit(solution)/shard_map/ppermute | solution.py:287
  164.6 3.8 %collective-permute-start.9 = (f32[256,512]{1,0:T(8,128)S(1)}, f32[256,512]{1,0:T(8,128)S(1)}, u32[]{:S(2)}, u32[]{:S(2)}) collective-permute-start(f32[256,512]{1,0:T(8,128)S(1)} %across_z_quotient.3.own), channel_id=1, source_target_pairs={{0,1},{1,0},{2,3},{3,2},{4,5},{5,4},{6,7},{7,6},{8,9},{9,8},{10,11... | collective-permute-start | bytes 1572872 | tf_op jit(solution)/shard_map/ppermute | solution.py:284
  169.1 15.2 %collective-permute-start.10 = (f32[240,512]{1,0:T(8,128)S(1)}, f32[240,512]{1,0:T(8,128)S(1)}, u32[]{:S(2)}, u32[]{:S(2)}) collective-permute-start(f32[240,512]{1,0:T(8,128)S(1)} %get-tuple-element.125), channel_id=1, source_target_pairs={{0,2},{2,4},{4,6},{6,8},{8,10},{10,12},{12,14},{14,16},{16,18},{18... | collective-permute-start | bytes 1474568 | tf_op jit(solution)/shard_map/ppermute | solution.py:286
  171.0 17.3 %collective-permute-start.11 = (f32[240,512]{1,0:T(8,128)S(1)}, f32[240,512]{1,0:T(8,128)S(1)}, u32[]{:S(2)}, u32[]{:S(2)}) collective-permute-start(f32[240,512]{1,0:T(8,128)S(1)} %get-tuple-element.127), channel_id=1, source_target_pairs={{2,0},{4,2},{6,4},{8,6},{10,8},{12,10},{14,12},{16,14},{18,16},{20... | collective-permute-start | bytes 1474568 | tf_op jit(solution)/shard_map/ppermute | solution.py:287

commit v2 on v1

--- a/solution.py
+++ b/solution.py
@@ -68,6 +68,7 @@
     far = pick(weights, 1, source - target + radius + side, (rows, cells))
     same = source == target
     edge_same, edge_plane = same[:, :edge], plane[:, :edge]
+    beyond = planes + radius
 
     def one_plane(at, carry):
         where = (pl.ds(pl.multiple_of(at * rows, rows), rows), slice(None))
@@ -76,10 +77,10 @@
         put(oh, ol, where, jnp.where(plane == at, far, zero))
         middle = pick(weights, 0, plane - at + radius, (rows, cells))
         put(zh, zl, where, jnp.where(same, middle, zero))
-        left = pick(weights, 0, edge_plane - at, (rows, edge))
-        put(lh, ll, where, jnp.where(edge_same, left, zero))
-        right = pick(weights, 0, edge_plane - at + (planes + radius), (rows, edge))
-        put(rh, rl, where, jnp.where(edge_same, right, zero))
+        below = pick(weights, 0, edge_plane - at + core[0] * beyond, (rows, edge))
+        put(lh, ll, where, jnp.where(edge_same, below, zero))
+        above = pick(weights, 0, edge_plane - at + (1 - core[0]) * beyond, (rows, edge))
+        put(rh, rl, where, jnp.where(edge_same, above, zero))
         return carry
 
     lax.fori_loop(0, planes, one_plane, 0)
@@ -198,25 +199,25 @@
     )(messages, view, order, *table[0:2])
 
 
-def across_y_kernel(edge, own, other, yh, yl, oh, ol, whole, head, tail):
-    result = product((yh[...], yl[...]), halves(own[...])) + product((oh[...], ol[...]), halves(other[...]))
-    whole[...] = result
-    head[...] = result[:edge]
-    tail[...] = result[result.shape[0] - edge:]
-
-
-def across_y(own, other, table, edge):
+def across_y_kernel(edge, core, own, other, yh, yl, oh, ol, whole, first, second):
+    whole[...] = product((yh[...], yl[...]), halves(own[...])) + product((oh[...], ol[...]), halves(other[...]))
+    inner = whole.shape[0] - edge
+    first[...] = whole[pl.ds(pl.multiple_of((1 - core[0]) * inner, inner), edge), :]
+    second[...] = whole[pl.ds(pl.multiple_of(core[0] * inner, inner), edge), :]
+
+
+def across_y(core, own, other, table, edge):
     whole = jax.ShapeDtypeStruct(own.shape, F32)
     piece = jax.ShapeDtypeStruct((edge, own.shape[1]), F32)
     return pl.pallas_call(
         functools.partial(across_y_kernel, edge),
         out_shape=[whole, piece, piece],
-        in_specs=vmem(6),
+        in_specs=[pl.BlockSpec(memory_space=pltpu.SMEM)] + vmem(6),
         out_specs=vmem(3),
         compiler_params=params(6),
         cost_estimate=cost(10**9, 3 * 10**6),
         name="across_y",
-    )(own, other, *table[2:6])
+    )(core, own, other, *table[2:6])
 
 
 def across_z_kernel(kind, left, own, right, zh, zl, lh, ll, rh, rl, factor, *rest):
@@ -276,15 +277,15 @@
     order = ordering(count_x, per_slab)
 
     swap = [(0, 1), (1, 0)]
-    up = [(i, i + 1) for i in range(slabs - 1)]
-    down = [(i + 1, i) for i in range(slabs - 1)]
+    up = [[(2 * i + core, 2 * i + 2 + core) for i in range(slabs - 1)] for core in range(2)]
+    down = [[(2 * i + 2 + core, 2 * i + core) for i in range(slabs - 1)] for core in range(2)]
 
     second, estimate, along_x = start(arrived, first, order, steps[0], planes)
     for step, table in enumerate(steps):
         other = lax.ppermute(along_x, "gy", swap)
-        whole, head, tail = across_y(along_x, other, table, edge)
-        left = lax.ppermute(tail, "gz", up)
-        right = lax.ppermute(head, "gz", down)
+        whole, before, after = across_y(core, along_x, other, table, edge)
+        left = lax.ppermute(before, ("gz", "gy"), up[0] + down[1])
+        right = lax.ppermute(after, ("gz", "gy"), down[0] + up[1])
         if step % 2 == 0:
             measured = first if step == 0 else second
             (along_x,) = across_z("quotient", left, whole, right, table, measured, steps[step + 1])

time: 190 us -> 182 us (0.958)
  waiting for transfers between devices: 83.8 us -> 75 us
    ppermute x8, waiting for transfers between devices: 47.6 us -> 38.8 us  [the longest x4 29 us: shards(): left = lax.ppermute(before, ('gz', 'gy'), up[0] + down[1])]
where the time goes in v2:
time: 182 us; the launch traced here: 181 us
  starting transfers between devices  83.1 us (46%)
  waiting for transfers between devices  75 us (41%)
  Pallas kernels  19.4 us (11%)
  local copies, waits for them, and re-layouts  3.59 us (2%)
    all_to_all x1, starting transfers between devices, shards(): lax.all_to_all(packed.reshape(slabs, -1, lanes), 'gz', 0, 0, tiled=True)  51.4 us
    ppermute x4, waiting for transfers between devices, shards(): left = lax.ppermute(before, ('gz', 'gy'), up[0] + down[1])  29 us
    all_to_all x1, waiting for transfers between devices, shards(): lax.all_to_all(packed.reshape(slabs, -1, lanes), 'gz', 0, 0, tiled=True)  28.7 us
    ppermute x4, starting transfers between devices, shards(): left = lax.ppermute(before, ('gz', 'gy'), up[0] + down[1])  14.4 us
    ppermute x4, waiting for transfers between devices, shards(): right = lax.ppermute(after, ('gz', 'gy'), down[0] + up[1])  9.78 us
    ppermute x4, starting transfers between devices, shards(): right = lax.ppermute(after, ('gz', 'gy'), down[0] + up[1])  9.48 us
    pallas_call x4, Pallas kernels, tables(): pl.pallas_call(functools.partial(tables_kernel, planes, rows, flipped), o...  8.66 us
    ppermute x4, starting transfers between devices, shards(): other = lax.ppermute(along_x, 'gy', swap)  7.8 us
  transfers between devices with their start and end apart: 13, of which 13 were waited for; matrix products, arithmetic and copies ran while one was open for 0% of the time, Pallas kernels for 5%

profile of v2, /device:TPU:94, one launch (start us, length us, event | category | flops | bytes accessed | tf_op | source)
XLA Modules:
  0.0 181.3 jit_solution(5281936764581602893)
XLA Ops:
  0.0 0.0 copy-start.1
  0.0 1.0 copy-done.1
  1.0 1.3 pack.1
  2.3 51.4 %all-to-all-start = ((f32[128,8,128]{2,1,0:T(8,128)}), f32[128,8,128]{2,1,0:T(8,128)S(1)}, u32[]{:S(2)}, u32[]{:S(2)}) async-start(f32[128,8,128]{2,1,0:T(8,128)} %bitcast.2), calls=%async_computation | async-start | bytes 1048576 | tf_op jit(solution)/shard_map/all_to_all | solution.py:268
  53.8 0.0 copy-start
  53.8 0.0 copy-start.2
  53.8 0.1 ordering.1.order
  53.9 0.6 copy-done.2
  54.5 2.2 %tables.4 = (bf16[512,512]{1,0:T(8,128)(2,1)S(1)}, bf16[512,512]{1,0:T(8,128)(2,1)S(1)}, bf16[256,256]{1,0:T(8,128)(2,1)S(1)}, bf16[256,256]{1,0:T(8,128)(2,1)S(...) custom-call(f32[3,31]{1,0:T(4,128)S(1)} %copy-done.2, ...), custom_call_target="tpu_custom_call" | custom-call | flops 10000000 | bytes 4000000 | tf_op jit(solution)/shard_map/tables/pallas_call | solution.py:106
  56.7 0.0 copy-start.4
  56.7 0.6 copy-done.4
  57.3 0.0 copy-start.6
  57.3 0.6 copy-done.6
  58.0 0.0 copy-start.8
  58.0 0.6 copy-done.8
  58.6 28.7 %all-to-all-done = f32[128,8,128]{2,1,0:T(8,128)S(1)} async-done(((f32[128,8,128]{2,1,0:T(8,128)}), f32[128,8,128]{2,1,0:T(8,128)S(1)}, u32[]{:S(2)}, u32[]{:S(2)}) %all-to-all-start) | async-done | bytes 524320 | tf_op jit(solution)/shard_map/all_to_all | solution.py:268
  87.4 0.0 copy-done
  87.4 0.0 copy-start.5
  87.4 0.0 copy-start.7
  87.4 0.0 copy-start.9
  87.4 1.3 start.1
  88.6 2.0 %collective-permute-start = (f32[256,512]{1,0:T(8,128)S(1)}, f32[256,512]{1,0:T(8,128)S(1)}, u32[]{:S(2)}, u32[]{:S(2)}) collective-permute-start(f32[256,512]{1,0:T(8,128)S(1)} %get-tuple-element.72.own), channel_id=1, source_target_pairs={{0,1},{1,0},{2,3},{3,2},{4,5},{5,4},{6,7},{7,6},{8,9},{9,8},{10,11... | collective-permute-start | bytes 1572872 | tf_op jit(solution)/shard_map/ppermute | solution.py:285
  90.6 1.9 %collective-permute-done.other = f32[256,512]{1,0:T(8,128)S(1)} collective-permute-done((f32[256,512]{1,0:T(8,128)S(1)}, f32[256,512]{1,0:T(8,128)S(1)}, u32[]{:S(2)}, u32[]{:S(2)}) %collective-permute-start) | collective-permute-done | bytes 524320 | tf_op jit(solution)/shard_map/ppermute | solution.py:285
  92.5 0.0 copy-done.5
  92.5 0.0 copy-done.7
  92.5 0.0 copy-done.9
  92.5 0.7 across_y.4
  93.2 3.2 %collective-permute-start.1 = (f32[240,512]{1,0:T(8,128)S(1)}, f32[240,512]{1,0:T(8,128)S(1)}, u32[]{:S(2)}, u32[]{:S(2)}) collective-permute-start(f32[240,512]{1,0:T(8,128)S(1)} %get-tuple-element.77), channel_id=1, source_target_pairs={{0,2},{2,4},{4,6},{6,8},{8,10},{10,12},{12,14},{14,16},{16,18},{18... | collective-permute-start | bytes 1474568 | tf_op jit(solution)/shard_map/ppermute | solution.py:287
  96.3 2.7 %collective-permute-start.2 = (f32[240,512]{1,0:T(8,128)S(1)}, f32[240,512]{1,0:T(8,128)S(1)}, u32[]{:S(2)}, u32[]{:S(2)}) collective-permute-start(f32[240,512]{1,0:T(8,128)S(1)} %get-tuple-element.79), channel_id=1, source_target_pairs={{2,0},{4,2},{6,4},{8,6},{10,8},{12,10},{14,12},{16,14},{18,16},{20... | collective-permute-start | bytes 1474568 | tf_op jit(solution)/shard_map/ppermute | solution.py:288
  99.1 2.2 %tables.5 = (bf16[512,512]{1,0:T(8,128)(2,1)S(1)}, bf16[512,512]{1,0:T(8,128)(2,1)S(1)}, bf16[256,256]{1,0:T(8,128)(2,1)S(1)}, bf16[256,256]{1,0:T(8,128)(2,1)S(...) custom-call(f32[3,31]{1,0:T(4,128)S(1)} %copy-done.2, ...), custom_call_target="tpu_custom_call" | custom-call | flops 10000000 | bytes 4000000 | tf_op jit(solution)/shard_map/tables/pallas_call | solution.py:106
  101.2 6.7 %collective-permute-done.1.left = f32[240,512]{1,0:T(8,128)S(1)} collective-permute-done((f32[240,512]{1,0:T(8,128)S(1)}, f32[240,512]{1,0:T(8,128)S(1)}, u32[]{:S(2)}, u32[]{:S(2)}) %collective-permute-start.1) | collective-permute-done | bytes 491552 | tf_op jit(solution)/shard_map/ppermute | solution.py:287
  107.9 2.5 %collective-permute-done.2.right = f32[240,512]{1,0:T(8,128)S(1)} collective-permute-done((f32[240,512]{1,0:T(8,128)S(1)}, f32[240,512]{1,0:T(8,128)S(1)}, u32[]{:S(2)}, u32[]{:S(2)}) %collective-permute-start.2) | collective-permute-done | bytes 491552 | tf_op jit(solution)/shard_map/ppermute | solution.py:288
  110.4 1.3 across_z_quotient.2.own
  111.7 2.0 %collective-permute-start.3 = (f32[256,512]{1,0:T(8,128)S(1)}, f32[256,512]{1,0:T(8,128)S(1)}, u32[]{:S(2)}, u32[]{:S(2)}) collective-permute-start(f32[256,512]{1,0:T(8,128)S(1)} %across_z_quotient.2.own), channel_id=1, source_target_pairs={{0,1},{1,0},{2,3},{3,2},{4,5},{5,4},{6,7},{7,6},{8,9},{9,8},{10,11... | collective-permute-start | bytes 1572872 | tf_op jit(solution)/shard_map/ppermute | solution.py:285
  113.7 1.9 %collective-permute-done.3.other = f32[256,512]{1,0:T(8,128)S(1)} collective-permute-done((f32[256,512]{1,0:T(8,128)S(1)}, f32[256,512]{1,0:T(8,128)S(1)}, u32[]{:S(2)}, u32[]{:S(2)}) %collective-permute-start.3) | collective-permute-done | bytes 524320 | tf_op jit(solution)/shard_map/ppermute | solution.py:285
  115.6 0.7 across_y.5
  116.2 0.0 copy-start.3
  116.3 3.5 %collective-permute-start.4 = (f32[240,512]{1,0:T(8,128)S(1)}, f32[240,512]{1,0:T(8,128)S(1)}, u32[]{:S(2)}, u32[]{:S(2)}) collective-permute-start(f32[240,512]{1,0:T(8,128)S(1)} %get-tuple-element.92), channel_id=1, source_target_pairs={{0,2},{2,4},{4,6},{6,8},{8,10},{10,12},{12,14},{14,16},{16,18},{18... | collective-permute-start | bytes 1474568 | tf_op jit(solution)/shard_map/ppermute | solution.py:287
  119.7 2.5 %collective-permute-start.5 = (f32[240,512]{1,0:T(8,128)S(1)}, f32[240,512]{1,0:T(8,128)S(1)}, u32[]{:S(2)}, u32[]{:S(2)}) collective-permute-start(f32[240,512]{1,0:T(8,128)S(1)} %get-tuple-element.94), channel_id=1, source_target_pairs={{2,0},{4,2},{6,4},{8,6},{10,8},{12,10},{14,12},{16,14},{18,16},{20... | collective-permute-start | bytes 1474568 | tf_op jit(solution)/shard_map/ppermute | solution.py:288
  122.2 0.0 copy-done.3
  122.2 2.2 %tables.6 = (bf16[512,512]{1,0:T(8,128)(2,1)S(1)}, bf16[512,512]{1,0:T(8,128)(2,1)S(1)}, bf16[256,256]{1,0:T(8,128)(2,1)S(1)}, bf16[256,256]{1,0:T(8,128)(2,1)S(...) custom-call(f32[3,31]{1,0:T(4,128)S(1)} %copy-done.3, ...), custom_call_target="tpu_custom_call" | custom-call | flops 10000000 | bytes 4000000 | tf_op jit(solution)/shard_map/tables/pallas_call | solution.py:106
  124.4 6.8 %collective-permute-done.4.left = f32[240,512]{1,0:T(8,128)S(1)} collective-permute-done((f32[240,512]{1,0:T(8,128)S(1)}, f32[240,512]{1,0:T(8,128)S(1)}, u32[]{:S(2)}, u32[]{:S(2)}) %collective-permute-start.4) | collective-permute-done | bytes 491552 | tf_op jit(solution)/shard_map/ppermute | solution.py:287
  131.1 2.4 %collective-permute-done.5.right = f32[240,512]{1,0:T(8,128)S(1)} collective-permute-done((f32[240,512]{1,0:T(8,128)S(1)}, f32[240,512]{1,0:T(8,128)S(1)}, u32[]{:S(2)}, u32[]{:S(2)}) %collective-permute-start.5) | collective-permute-done | bytes 491552 | tf_op jit(solution)/shard_map/ppermute | solution.py:288
  133.6 1.3 across_z_update.1
  134.8 2.0 %collective-permute-start.6 = (f32[256,512]{1,0:T(8,128)S(1)}, f32[256,512]{1,0:T(8,128)S(1)}, u32[]{:S(2)}, u32[]{:S(2)}) collective-permute-start(f32[256,512]{1,0:T(8,128)S(1)} %get-tuple-element.104.own), channel_id=1, source_target_pairs={{0,1},{1,0},{2,3},{3,2},{4,5},{5,4},{6,7},{7,6},{8,9},{9,8},{10,11... | collective-permute-start | bytes 1572872 | tf_op jit(solution)/shard_map/ppermute | solution.py:285
  136.8 1.9 %collective-permute-done.6.other = f32[256,512]{1,0:T(8,128)S(1)} collective-permute-done((f32[256,512]{1,0:T(8,128)S(1)}, f32[256,512]{1,0:T(8,128)S(1)}, u32[]{:S(2)}, u32[]{:S(2)}) %collective-permute-start.6) | collective-permute-done | bytes 524320 | tf_op jit(solution)/shard_map/ppermute | solution.py:285
  138.7 0.7 across_y.6
  139.3 3.7 %collective-permute-start.7 = (f32[240,512]{1,0:T(8,128)S(1)}, f32[240,512]{1,0:T(8,128)S(1)}, u32[]{:S(2)}, u32[]{:S(2)}) collective-permute-start(f32[240,512]{1,0:T(8,128)S(1)} %get-tuple-element.109), channel_id=1, source_target_pairs={{0,2},{2,4},{4,6},{6,8},{8,10},{10,12},{12,14},{14,16},{16,18},{18... | collective-permute-start | bytes 1474568 | tf_op jit(solution)/shard_map/ppermute | solution.py:287
  143.1 2.3 %collective-permute-start.8 = (f32[240,512]{1,0:T(8,128)S(1)}, f32[240,512]{1,0:T(8,128)S(1)}, u32[]{:S(2)}, u32[]{:S(2)}) collective-permute-start(f32[240,512]{1,0:T(8,128)S(1)} %get-tuple-element.111), channel_id=1, source_target_pairs={{2,0},{4,2},{6,4},{8,6},{10,8},{12,10},{14,12},{16,14},{18,16},{20... | collective-permute-start | bytes 1474568 | tf_op jit(solution)/shard_map/ppermute | solution.py:288
  145.4 2.2 %tables.7 = (bf16[512,512]{1,0:T(8,128)(2,1)S(1)}, bf16[512,512]{1,0:T(8,128)(2,1)S(1)}, bf16[256,256]{1,0:T(8,128)(2,1)S(1)}, bf16[256,256]{1,0:T(8,128)(2,1)S(...) custom-call(f32[3,31]{1,0:T(4,128)S(1)} %copy-done.3, ...), custom_call_target="tpu_custom_call" | custom-call | flops 10000000 | bytes 4000000 | tf_op jit(solution)/shard_map/tables/pallas_call | solution.py:106
  147.6 6.6 %collective-permute-done.7.left = f32[240,512]{1,0:T(8,128)S(1)} collective-permute-done((f32[240,512]{1,0:T(8,128)S(1)}, f32[240,512]{1,0:T(8,128)S(1)}, u32[]{:S(2)}, u32[]{:S(2)}) %collective-permute-start.7) | collective-permute-done | bytes 491552 | tf_op jit(solution)/shard_map/ppermute | solution.py:287
  154.2 2.4 %collective-permute-done.8.right = f32[240,512]{1,0:T(8,128)S(1)} collective-permute-done((f32[240,512]{1,0:T(8,128)S(1)}, f32[240,512]{1,0:T(8,128)S(1)}, u32[]{:S(2)}, u32[]{:S(2)}) %collective-permute-start.8) | collective-permute-done | bytes 491552 | tf_op jit(solution)/shard_map/ppermute | solution.py:288
  156.6 1.3 across_z_quotient.3.own
  158.0 2.0 %collective-permute-start.9 = (f32[256,512]{1,0:T(8,128)S(1)}, f32[256,512]{1,0:T(8,128)S(1)}, u32[]{:S(2)}, u32[]{:S(2)}) collective-permute-start(f32[256,512]{1,0:T(8,128)S(1)} %across_z_quotient.3.own), channel_id=1, source_target_pairs={{0,1},{1,0},{2,3},{3,2},{4,5},{5,4},{6,7},{7,6},{8,9},{9,8},{10,11... | collective-permute-start | bytes 1572872 | tf_op jit(solution)/shard_map/ppermute | solution.py:285
  159.9 1.9 %collective-permute-done.9.other = f32[256,512]{1,0:T(8,128)S(1)} collective-permute-done((f32[256,512]{1,0:T(8,128)S(1)}, f32[256,512]{1,0:T(8,128)S(1)}, u32[]{:S(2)}, u32[]{:S(2)}) %collective-permute-start.9) | collective-permute-done | bytes 524320 | tf_op jit(solution)/shard_map/ppermute | solution.py:285
  161.8 0.7 across_y.7
  162.5 4.0 %collective-permute-start.10 = (f32[240,512]{1,0:T(8,128)S(1)}, f32[240,512]{1,0:T(8,128)S(1)}, u32[]{:S(2)}, u32[]{:S(2)}) collective-permute-start(f32[240,512]{1,0:T(8,128)S(1)} %get-tuple-element.125), channel_id=1, source_target_pairs={{0,2},{2,4},{4,6},{6,8},{8,10},{10,12},{12,14},{14,16},{16,18},{18... | collective-permute-start | bytes 1474568 | tf_op jit(solution)/shard_map/ppermute | solution.py:287
  166.5 2.0 %collective-permute-start.11 = (f32[240,512]{1,0:T(8,128)S(1)}, f32[240,512]{1,0:T(8,128)S(1)}, u32[]{:S(2)}, u32[]{:S(2)}) collective-permute-start(f32[240,512]{1,0:T(8,128)S(1)} %get-tuple-element.127), channel_id=1, source_target_pairs={{2,0},{4,2},{6,4},{8,6},{10,8},{12,10},{14,12},{16,14},{18,16},{20... | collective-permute-start | bytes 1474568 | tf_op jit(solution)/shard_map/ppermute | solution.py:288
  168.4 8.9 %collective-permute-done.10.left = f32[240,512]{1,0:T(8,128)S(1)} collective-permute-done((f32[240,512]{1,0:T(8,128)S(1)}, f32[240,512]{1,0:T(8,128)S(1)}, u32[]{:S(2)}, u32[]{:S(2)}) %collective-permute-start.10) | collective-permute-done | bytes 491552 | tf_op jit(solution)/shard_map/ppermute | solution.py:287
  177.3 2.4 %collective-permute-done.11.right = f32[240,512]{1,0:T(8,128)S(1)} collective-permute-done((f32[240,512]{1,0:T(8,128)S(1)}, f32[240,512]{1,0:T(8,128)S(1)}, u32[]{:S(2)}, u32[]{:S(2)}) %collective-permute-start.11) | collective-permute-done | bytes 491552 | tf_op jit(solution)/shard_map/ppermute | solution.py:288
  179.8 1.6 across_z_last.1
Async XLA Ops:
  0.0 1.0 copy-start.1
  2.3 85.0 %all-to-all-start = ((f32[128,8,128]{2,1,0:T(8,128)}), f32[128,8,128]{2,1,0:T(8,128)S(1)}, u32[]{:S(2)}, u32[]{:S(2)}) async-start(f32[128,8,128]{2,1,0:T(8,128)} %bitcast.2), calls=%async_computation | async-start | bytes 1048576 | tf_op jit(solution)/shard_map/all_to_all | solution.py:268
  53.8 33.6 %copy-start = (f32[16,16,512]{2,1,0:T(8,128)S(1)}, f32[16,16,512]{2,1,0:T(8,128)}, u32[]{:S(2)}) copy-start(f32[16,16,512]{2,1,0:T(8,128)} %param.4) | copy-start | bytes 1572868
  53.8 0.7 copy-start.2
  56.7 0.7 copy-start.4
  57.3 0.6 copy-start.6
  58.0 0.7 copy-start.8
  87.4 5.1 %copy-start.5 = (bf16[256,256]{1,0:T(8,128)(2,1)S(1)}, bf16[256,256]{1,0:T(8,128)(2,1)}, u32[]{:S(2)}) copy-start(bf16[256,256]{1,0:T(8,128)(2,1)} %copy-done.4) | copy-start | bytes 393220
  87.4 5.1 %copy-start.7 = (bf16[256,256]{1,0:T(8,128)(2,1)S(1)}, bf16[256,256]{1,0:T(8,128)(2,1)}, u32[]{:S(2)}) copy-start(bf16[256,256]{1,0:T(8,128)(2,1)} %copy-done.6) | copy-start | bytes 393220
  87.4 5.1 %copy-start.9 = (bf16[256,256]{1,0:T(8,128)(2,1)S(1)}, bf16[256,256]{1,0:T(8,128)(2,1)}, u32[]{:S(2)}) copy-start(bf16[256,256]{1,0:T(8,128)(2,1)} %copy-done.8) | copy-start | bytes 393220
  88.6 3.8 %collective-permute-start = (f32[256,512]{1,0:T(8,128)S(1)}, f32[256,512]{1,0:T(8,128)S(1)}, u32[]{:S(2)}, u32[]{:S(2)}) collective-permute-start(f32[256,512]{1,0:T(8,128)S(1)} %get-tuple-element.72.own), channel_id=1, source_target_pairs={{0,1},{1,0},{2,3},{3,2},{4,5},{5,4},{6,7},{7,6},{8,9},{9,8},{10,11... | collective-permute-start | bytes 1572872 | tf_op jit(solution)/shard_map/ppermute | solution.py:285
  93.2 14.7 %collective-permute-start.1 = (f32[240,512]{1,0:T(8,128)S(1)}, f32[240,512]{1,0:T(8,128)S(1)}, u32[]{:S(2)}, u32[]{:S(2)}) collective-permute-start(f32[240,512]{1,0:T(8,128)S(1)} %get-tuple-element.77), channel_id=1, source_target_pairs={{0,2},{2,4},{4,6},{6,8},{8,10},{10,12},{12,14},{14,16},{16,18},{18... | collective-permute-start | bytes 1474568 | tf_op jit(solution)/shard_map/ppermute | solution.py:287
  96.3 14.1 %collective-permute-start.2 = (f32[240,512]{1,0:T(8,128)S(1)}, f32[240,512]{1,0:T(8,128)S(1)}, u32[]{:S(2)}, u32[]{:S(2)}) collective-permute-start(f32[240,512]{1,0:T(8,128)S(1)} %get-tuple-element.79), channel_id=1, source_target_pairs={{2,0},{4,2},{6,4},{8,6},{10,8},{12,10},{14,12},{16,14},{18,16},{20... | collective-permute-start | bytes 1474568 | tf_op jit(solution)/shard_map/ppermute | solution.py:288
  111.7 3.8 %collective-permute-start.3 = (f32[256,512]{1,0:T(8,128)S(1)}, f32[256,512]{1,0:T(8,128)S(1)}, u32[]{:S(2)}, u32[]{:S(2)}) collective-permute-start(f32[256,512]{1,0:T(8,128)S(1)} %across_z_quotient.2.own), channel_id=1, source_target_pairs={{0,1},{1,0},{2,3},{3,2},{4,5},{5,4},{6,7},{7,6},{8,9},{9,8},{10,11... | collective-permute-start | bytes 1572872 | tf_op jit(solution)/shard_map/ppermute | solution.py:285
  116.2 5.9 %copy-start.3 = (f32[3,31]{1,0:T(4,128)S(1)}, f32[3,31]{1,0:T(4,128)}, u32[]{:S(2)}) copy-start(f32[3,31]{1,0:T(4,128)} %spread_ref.7) | copy-start | bytes 1120
  116.3 14.9 %collective-permute-start.4 = (f32[240,512]{1,0:T(8,128)S(1)}, f32[240,512]{1,0:T(8,128)S(1)}, u32[]{:S(2)}, u32[]{:S(2)}) collective-permute-start(f32[240,512]{1,0:T(8,128)S(1)} %get-tuple-element.92), channel_id=1, source_target_pairs={{0,2},{2,4},{4,6},{6,8},{8,10},{10,12},{12,14},{14,16},{16,18},{18... | collective-permute-start | bytes 1474568 | tf_op jit(solution)/shard_map/ppermute | solution.py:287
  119.7 13.8 %collective-permute-start.5 = (f32[240,512]{1,0:T(8,128)S(1)}, f32[240,512]{1,0:T(8,128)S(1)}, u32[]{:S(2)}, u32[]{:S(2)}) collective-permute-start(f32[240,512]{1,0:T(8,128)S(1)} %get-tuple-element.94), channel_id=1, source_target_pairs={{2,0},{4,2},{6,4},{8,6},{10,8},{12,10},{14,12},{16,14},{18,16},{20... | collective-permute-start | bytes 1474568 | tf_op jit(solution)/shard_map/ppermute | solution.py:288
  134.8 3.8 %collective-permute-start.6 = (f32[256,512]{1,0:T(8,128)S(1)}, f32[256,512]{1,0:T(8,128)S(1)}, u32[]{:S(2)}, u32[]{:S(2)}) collective-permute-start(f32[256,512]{1,0:T(8,128)S(1)} %get-tuple-element.104.own), channel_id=1, source_target_pairs={{0,1},{1,0},{2,3},{3,2},{4,5},{5,4},{6,7},{7,6},{8,9},{9,8},{10,11... | collective-permute-start | bytes 1572872 | tf_op jit(solution)/shard_map/ppermute | solution.py:285
  139.3 14.9 %collective-permute-start.7 = (f32[240,512]{1,0:T(8,128)S(1)}, f32[240,512]{1,0:T(8,128)S(1)}, u32[]{:S(2)}, u32[]{:S(2)}) collective-permute-start(f32[240,512]{1,0:T(8,128)S(1)} %get-tuple-element.109), channel_id=1, source_target_pairs={{0,2},{2,4},{4,6},{6,8},{8,10},{10,12},{12,14},{14,16},{16,18},{18... | collective-permute-start | bytes 1474568 | tf_op jit(solution)/shard_map/ppermute | solution.py:287
  143.1 13.6 %collective-permute-start.8 = (f32[240,512]{1,0:T(8,128)S(1)}, f32[240,512]{1,0:T(8,128)S(1)}, u32[]{:S(2)}, u32[]{:S(2)}) collective-permute-start(f32[240,512]{1,0:T(8,128)S(1)} %get-tuple-element.111), channel_id=1, source_target_pairs={{2,0},{4,2},{6,4},{8,6},{10,8},{12,10},{14,12},{16,14},{18,16},{20... | collective-permute-start | bytes 1474568 | tf_op jit(solution)/shard_map/ppermute | solution.py:288
  158.0 3.8 %collective-permute-start.9 = (f32[256,512]{1,0:T(8,128)S(1)}, f32[256,512]{1,0:T(8,128)S(1)}, u32[]{:S(2)}, u32[]{:S(2)}) collective-permute-start(f32[256,512]{1,0:T(8,128)S(1)} %across_z_quotient.3.own), channel_id=1, source_target_pairs={{0,1},{1,0},{2,3},{3,2},{4,5},{5,4},{6,7},{7,6},{8,9},{9,8},{10,11... | collective-permute-start | bytes 1572872 | tf_op jit(solution)/shard_map/ppermute | solution.py:285
  162.5 14.9 %collective-permute-start.10 = (f32[240,512]{1,0:T(8,128)S(1)}, f32[240,512]{1,0:T(8,128)S(1)}, u32[]{:S(2)}, u32[]{:S(2)}) collective-permute-start(f32[240,512]{1,0:T(8,128)S(1)} %get-tuple-element.125), channel_id=1, source_target_pairs={{0,2},{2,4},{4,6},{6,8},{8,10},{10,12},{12,14},{14,16},{16,18},{18... | collective-permute-start | bytes 1474568 | tf_op jit(solution)/shard_map/ppermute | solution.py:287
  166.5 13.3 %collective-permute-start.11 = (f32[240,512]{1,0:T(8,128)S(1)}, f32[240,512]{1,0:T(8,128)S(1)}, u32[]{:S(2)}, u32[]{:S(2)}) collective-permute-start(f32[240,512]{1,0:T(8,128)S(1)} %get-tuple-element.127), channel_id=1, source_target_pairs={{2,0},{4,2},{6,4},{8,6},{10,8},{12,10},{14,12},{16,14},{18,16},{20... | collective-permute-start | bytes 1474568 | tf_op jit(solution)/shard_map/ppermute | solution.py:288

commit v3 on v1

v3 whole, which is shorter than its diff:
```python
import functools

import jax
import jax.numpy as jnp
from jax import lax
from jax.experimental import pallas as pl
from jax.experimental.pallas import tpu as pltpu
from jax.sharding import PartitionSpec as P


BF16 = jnp.bfloat16
F32 = jnp.float32
MIB = 1 << 20


def halves(values):
    high = values.astype(BF16)
    low = (values - high.astype(F32)).astype(BF16)
    return high, low


def product(left, right):
    dot = functools.partial(jnp.dot, preferred_element_type=F32)
    return dot(left[0], right[0]) + (dot(left[0], right[1]) + dot(left[1], right[0]))


def pick(weights, axis, place):
    spread, flipped = weights
    taps = spread.shape[1]
    table = jnp.zeros(place.shape, F32)
    total = jnp.zeros((1, 1), F32)
    for tap in range(taps):
        value = spread[axis, taps - 1 - tap if flipped else tap]
        table = jnp.where(place == tap, value, table)
        total = total + value
    return table / total


def put(high_ref, low_ref, where, values):
    high, low = halves(values)
    high_ref[where] = high
    low_ref[where] = low


SHIFTS = ((0, 0), (1, -1), (2, -2), (-1, 1), (None, 2))


def tables_kernel(planes, rows, flipped, spread_ref, core, xh, xl, yh, yl, *zs):
    weights = (spread_ref, flipped)
    radius = spread_ref.shape[1] // 2
    count_x = xh.shape[0]
    lane = 128
    spread = lax.broadcasted_iota(jnp.int32, (lane, lane), 0) - lax.broadcasted_iota(jnp.int32, (lane, lane), 1)
    blocks = {shift: halves(pick(weights, 2, spread + (radius + shift * lane))) for shift in (-1, 0, 1)}
    nothing = jnp.zeros((lane, lane), BF16)
    for row in range(count_x // lane):
        for column in range(count_x // lane):
            where = (slice(row * lane, (row + 1) * lane), slice(column * lane, (column + 1) * lane))
            high, low = blocks.get(row - column, (nothing, nothing))
            xh[where] = high
            xl[where] = low
    half = planes // 2
    count = half * rows
    zero = jnp.zeros((), F32)

    def places(length, shape):
        column = lax.broadcasted_iota(jnp.int32, shape, 1)
        return column // length, (column % length) // rows, column % rows

    target = lax.broadcasted_iota(jnp.int32, (rows, 2 * count), 0)
    part, plane, cell = places(count, (rows, 2 * count))
    across = [pick(weights, 1, rows * (part - side) + cell - target + radius) for side in range(2)]
    pieces = []
    for position, (south, north) in enumerate(SHIFTS):
        length = zs[2 * position].shape[1] // 2
        base = radius * -1 if south is None else south * half
        shift = jnp.where(core[0] == 0, base, north * half)
        side_of, _, cell_of = places(length, (rows, 2 * length))
        same = cell_of == lax.broadcasted_iota(jnp.int32, (rows, 2 * length), 0)
        near = places(length, (8, 2 * length))[1] + (shift + radius)
        pieces.append((zs[2 * position], zs[2 * position + 1], near, side_of, same))

    def one_plane(at, carry):
        values = [pick(weights, 0, near - at) for _, _, near, _, _ in pieces]
        for side in range(2):
            where = (pl.ds(pl.multiple_of(side * count + at * rows, rows), rows), slice(None))
            put(yh, yl, where, jnp.where(plane == at, across[side], zero))
            for (high, low, _, side_of, same), value in zip(pieces, values):
                spread_out = jnp.concatenate([value] * (rows // 8), axis=0)
                put(high, low, where, jnp.where(same & (side_of == side), spread_out, zero))
        return carry

    lax.fori_loop(0, half, one_plane, 0)


def vmem(count):
    return [pl.BlockSpec(memory_space=pltpu.VMEM)] * count


def smem(count):
    return [pl.BlockSpec(memory_space=pltpu.SMEM)] * count


def params(mib):
    return pltpu.CompilerParams(vmem_limit_bytes=mib * MIB)


def cost(flops, moved):
    return pl.CostEstimate(flops=flops, bytes_accessed=moved, transcendentals=0)


def tables(spread, flipped, core, planes, rows, count_x):
    cells = planes * rows
    short = 2 * (spread.shape[1] // 2 - planes // 2) * rows
    shapes = [(count_x, count_x)] + [(cells, cells)] * 5 + [(cells, short)]
    out = [jax.ShapeDtypeStruct(shape, BF16) for shape in shapes for _ in range(2)]
    return pl.pallas_call(
        functools.partial(tables_kernel, planes, rows, flipped),
        out_shape=out,
        in_specs=smem(2),
        out_specs=vmem(len(out)),
        compiler_params=params(6),
        cost_estimate=cost(10**7, 4 * 10**6),
        name="tables",
    )(spread, core)


def pack_kernel(planes, own, messages):
    lane = 128
    half = planes // 2
    for block in range(own.shape[1] // lane):
        turned = own[:, block * lane:(block + 1) * lane].T
        for slab in range(lane // planes):
            at = slab * planes
            tile = jnp.concatenate([turned[at:at + half], turned[at + half:at + planes]], axis=1)
            to = block * (lane // planes) + slab
            messages[to * half:(to + 1) * half, :] = tile


def pack(own, planes):
    per_slab, rows, count_z = own.shape
    return pl.pallas_call(
        functools.partial(pack_kernel, planes),
        out_shape=jax.ShapeDtypeStruct((count_z // 2, 2 * per_slab * rows), F32),
        in_specs=vmem(1),
        out_specs=vmem(1)[0],
        compiler_params=params(4),
        cost_estimate=cost(10**6, 10**6),
        name="pack",
    )(own.reshape(per_slab * rows, count_z))


def order_kernel(per_slab, order):
    count_x = order.shape[0]
    slabs = count_x // per_slab
    source = lax.broadcasted_iota(jnp.int32, order.shape, 0)
    target = lax.broadcasted_iota(jnp.int32, order.shape, 1)
    wanted = count_x - 1 - (per_slab * (source % slabs) + source // slabs)
    order[...] = jnp.where(target == wanted, F32(1.0), F32(0.0)).astype(BF16)


def ordering(count_x, per_slab):
    return pl.pallas_call(
        functools.partial(order_kernel, per_slab),
        out_shape=jax.ShapeDtypeStruct((count_x, count_x), BF16),
        out_specs=vmem(1)[0],
        compiler_params=params(4),
        cost_estimate=cost(10**6, 10**6),
        name="ordering",
    )()


def parted(core, values_ref, keep, give):
    count = keep.shape[0]
    keep[...] = values_ref[pl.ds(pl.multiple_of(core[0] * count, count), count), :]
    give[...] = values_ref[pl.ds(pl.multiple_of((1 - core[0]) * count, count), count), :]


def joined(core, keep, got, values_ref):
    count = keep.shape[0]
    values_ref[pl.ds(pl.multiple_of(core[0] * count, count), count), :] = keep[...]
    values_ref[pl.ds(pl.multiple_of((1 - core[0]) * count, count), count), :] = got[...]


def call(kernel, scalars, operands, shapes, scratch=()):
    return pl.pallas_call(
        kernel,
        out_shape=[jax.ShapeDtypeStruct(shape, F32) for shape in shapes],
        in_specs=smem(len(scalars)) + vmem(len(operands)),
        out_specs=vmem(len(shapes)),
        scratch_shapes=[pltpu.VMEM(shape, F32) for shape in scratch],
        compiler_params=params(6),
        cost_estimate=cost(10**9, 3 * 10**6),
    )(*scalars, *operands)


def start_kernel(planes, per_slab, core, messages, view, order, xh, xl, kept, given, kept_x, given_x, gathered, whole):
    half = planes // 2
    rows = view.shape[0] // planes
    slabs = messages.shape[0] // half
    for z in range(half):
        turned = messages[pl.ds(z, slabs, stride=half), :].T
        for part in range(2):
            for x in range(per_slab):
                at = (part * per_slab + x) * rows
                to = (part * half + z) * rows
                gathered[to:to + rows, x * slabs:(x + 1) * slabs] = turned[at:at + rows]
    values = gathered[...]
    high = values.astype(BF16)
    rest = values - high.astype(F32)
    middle = rest.astype(BF16)
    low = (rest - middle.astype(F32)).astype(BF16)
    dot = functools.partial(jnp.dot, preferred_element_type=F32)
    moved = (dot(high, order[...]) + dot(middle, order[...])) + dot(low, order[...])
    whole[...] = moved
    parted(core, whole, kept, given)
    whole[...] = product(halves(0.5 * (view[...] + moved)), (xh[...], xl[...]))
    parted(core, whole, kept_x, given_x)


def part_kernel(core, values, keep, give):
    parted(core, values, keep, give)


def join_kernel(core, keep, got, values):
    joined(core, keep, got, values)


def join_both_kernel(core, keep, got, view, values, estimate):
    joined(core, keep, got, values)
    estimate[...] = 0.5 * (view[...] + values[...])


def send_y(core, values, yh, yl, whole, second):
    whole[...] = product((yh[...], yl[...]), halves(values))
    count = whole.shape[0] // 2
    length = second.shape[0] // 2
    skipped = (1 - core[0]) * (count - length)
    for side in range(2):
        at = pl.multiple_of(side * count + skipped, count - length)
        second[side * length:(side + 1) * length, :] = whole[pl.ds(at, length), :]


def enter_kernel(core, keep, got, yh, yl, whole, second, values):
    joined(core, keep, got, values)
    send_y(core, values[...], yh, yl, whole, second)


def partial_kernel(pieces, *refs):
    total = None
    for piece in range(pieces):
        high, low, values = refs[3 * piece:3 * piece + 3]
        term = product((high[...], low[...]), halves(values[...]))
        total = term if total is None else total + term
    for more in refs[3 * pieces:-1]:
        total = total + more[...]
    refs[-1][...] = total


def partial(terms, more=()):
    operands = [operand for high, low, values in terms for operand in (high, low, values)]
    return call(functools.partial(partial_kernel, len(terms)), (), [*operands, *more], [terms[0][2].shape])[0]


def finish_kernel(kind, core, part, second, sh, sl, factor, *rest):
    blurred = part[...] + product((sh[...], sl[...]), halves(second[...]))
    if kind == "last":
        keep, give, values = rest
        values[...] = factor[...] * blurred
        parted(core, values, keep, give)
        return
    xh, xl, yh, yl, *outs = rest
    if kind == "quotient":
        value = factor[...] / blurred
    else:
        value = factor[...] * blurred
        outs[0][...] = value
    along_x = product(halves(value), (xh[...], xl[...]))
    send_y(core, along_x, yh, yl, outs[-2], outs[-1])


def finish(kind, core, part, second, table, factor, following):
    operands = [part, second, *table[12:14], factor]
    block = part.shape
    if kind == "last":
        piece = (block[0] // 2, block[1])
        shapes, scratch = [piece, piece], [block]
    else:
        operands += following[0:4]
        shapes, scratch = [block, second.shape], []
        if kind == "update":
            shapes = [block] + shapes
    return call(functools.partial(finish_kernel, kind), [core], operands, shapes, scratch)


def shards(view_a, view_b_own, spread_a, spread_b):
    planes, rows, count_x = view_a.shape
    cells = planes * rows
    short = 2 * (spread_a.shape[1] // 2 - planes // 2) * rows
    slabs = lax.axis_size("gz")
    per_slab = view_b_own.shape[0]
    first_y = view_a.reshape(cells, count_x)
    block, piece, ends = (cells, count_x), (cells // 2, count_x), (short, count_x)

    core = lax.axis_index("gy").astype(jnp.int32).reshape(1)
    swap = [(0, 1), (1, 0)]
    up = [[(2 * i + core, 2 * i + 2 + core) for i in range(slabs - 1)] for core in range(2)]
    down = [[(2 * i + 2 + core, 2 * i + core) for i in range(slabs - 1)] for core in range(2)]

    def table_of(step):
        return tables((spread_a, spread_b)[step // 2], step % 2 == 1, core, planes, rows, count_x)

    packed = pack(view_b_own, planes)
    lanes = packed.shape[1]
    arrived = lax.all_to_all(packed.reshape(slabs, -1, lanes), "gz", 0, 0, tiled=True)
    arrived = arrived.reshape(-1, lanes)
    keep, give = call(part_kernel, [core], [first_y], [piece, piece])
    got = lax.ppermute(give, "gy", swap)
    (first,) = call(join_kernel, [core], [keep, got], [block])
    table = table_of(0)
    order = ordering(count_x, per_slab)

    kept, given, kept_x, given_x = call(
        functools.partial(start_kernel, planes, per_slab), [core],
        [arrived, first_y, order, *table[0:2]], [piece] * 4, [block, block],
    )
    got_x = lax.ppermute(given_x, "gy", swap)
    whole, ends_of = call(enter_kernel, [core], [kept_x, got_x, *table[2:4]], [block, ends], [block])

    for step in range(4):
        first_planes = lax.ppermute(whole, ("gz", "gy"), up[1] + down[0])
        side_planes = lax.ppermute(whole, "gy", swap)
        second_planes = lax.ppermute(ends_of, ("gz", "gy"), up[0] + down[1])
        if step < 3:
            following = table_of(step + 1)
        part = partial([(*table[4:6], whole), (*table[6:8], side_planes)])
        forward_planes = lax.ppermute(first_planes, "gy", swap)
        part = partial([(*table[8:10], first_planes)], [part])
        if step == 0:
            got_b = lax.ppermute(given, "gy", swap)
            second, estimate = call(join_both_kernel, [core], [kept, got_b, first], [block, block])
        part = partial([(*table[10:12], forward_planes)], [part])
        arrivals = (core, part, second_planes, table)
        if step % 2 == 0:
            measured = first if step == 0 else second
            whole, ends_of = finish("quotient", *arrivals, measured, following)
        elif step < 3:
            estimate, whole, ends_of = finish("update", *arrivals, estimate, following)
        else:
            keep, give = finish("last", *arrivals, estimate, None)
        table = following
    got = lax.ppermute(give, "gy", swap)
    (estimate,) = call(join_kernel, [core], [keep, got], [block])
    return estimate.reshape(planes, rows, count_x)


def solution(mesh):
    in_specs = (P(("blocks", "gz"), "gy", None), P(("blocks", "gz"), "gy", None), P(), P())
    out_specs = P(("blocks", "gz"), "gy", None)
    return jax.shard_map(shards, mesh=mesh, in_specs=in_specs, out_specs=out_specs, check_vma=False)
```

time: 190 us -> 206 us (1.084)
  starting transfers between devices: 83 us -> 99.4 us
  waiting for transfers between devices: 83.8 us -> 77 us
  Pallas kernels: 19.2 us -> 21.8 us
  local copies, waits for them, and re-layouts: 3.59 us -> 5.84 us
    ppermute x12 -> x20, starting transfers between devices: 31.6 us -> 47.9 us  [the longest x4 12.8 us: shards(): side_planes = lax.ppermute(whole, 'gy', swap)]
    ppermute x12 -> x20, waiting for transfers between devices: 55.1 us -> 49.4 us  [the longest x4 27.8 us: shards(): first_planes = lax.ppermute(whole, ('gz', 'gy'), up[1] + down[0])]
    pallas_call x9 -> x22, Pallas kernels: 9.19 us -> 12.5 us  [call(): pl.pallas_call(kernel, out_shape=[jax.ShapeDtypeStruct(shape, F32) for sh...]
    unnamed x20 -> x28, local copies, waits for them, and re-layouts: 3.59 us -> 5.84 us
  transfers between devices with their start and end apart: 13 -> 21, of which waited for: 13 -> 11; matrix products, arithmetic and copies ran while one was open for 0% -> 0% of each run, Pallas kernels for 5% -> 7%
where the time goes in v3:
time: 206 us; the launch traced here: 204 us
  starting transfers between devices  99.4 us (48%)
  waiting for transfers between devices  77 us (37%)
  Pallas kernels  21.8 us (11%)
  local copies, waits for them, and re-layouts  5.84 us (3%)
    all_to_all x1, starting transfers between devices, shards(): lax.all_to_all(packed.reshape(slabs, -1, lanes), 'gz', 0, 0, tiled=True)  51.4 us
    ppermute x4, waiting for transfers between devices, shards(): first_planes = lax.ppermute(whole, ('gz', 'gy'), up[1] + down[0])  27.8 us
    all_to_all x1, waiting for transfers between devices, shards(): lax.all_to_all(packed.reshape(slabs, -1, lanes), 'gz', 0, 0, tiled=True)  27.6 us
    ppermute x4, waiting for transfers between devices, shards(): second_planes = lax.ppermute(ends_of, ('gz', 'gy'), up[0] + down[1])  18.9 us
    ppermute x4, starting transfers between devices, shards(): side_planes = lax.ppermute(whole, 'gy', swap)  12.8 us
    pallas_call x22, Pallas kernels, call(): pl.pallas_call(kernel, out_shape=[jax.ShapeDtypeStruct(shape, F32) for sh...  12.5 us
    ppermute x4, starting transfers between devices, shards(): second_planes = lax.ppermute(ends_of, ('gz', 'gy'), up[0] + down[1])  9.92 us
    ppermute x4, starting transfers between devices, shards(): first_planes = lax.ppermute(whole, ('gz', 'gy'), up[1] + down[0])  8.23 us
  transfers between devices with their start and end apart: 21, of which 11 were waited for; matrix products, arithmetic and copies ran while one was open for 0% of the time, Pallas kernels for 7%

profile of v3, /device:TPU:94, one launch (start us, length us, event | category | flops | bytes accessed | tf_op | source)
XLA Modules:
  0.0 204.5 jit_solution(10216440188819081889)
XLA Ops:
  0.0 1.0 copy-done
  1.0 1.3 pack.1
  2.3 51.4 %all-to-all-start = ((f32[128,8,128]{2,1,0:T(8,128)}), f32[128,8,128]{2,1,0:T(8,128)S(1)}, u32[]{:S(2)}, u32[]{:S(2)}) async-start(f32[128,8,128]{2,1,0:T(8,128)} %bitcast.2), calls=%async_computation | async-start | bytes 1048576 | tf_op jit(solution)/shard_map/all_to_all | solution.py:315
  53.9 0.6 copy-done.2
  54.5 1.9 tables.7
  56.5 0.6 copy-done.4
  57.1 0.7 copy-done.6
  57.8 0.6 copy-done.8
  58.4 0.7 copy-done.10
  59.1 0.6 copy-done.12
  59.7 27.6 %all-to-all-done = f32[128,8,128]{2,1,0:T(8,128)S(1)} async-done(((f32[128,8,128]{2,1,0:T(8,128)}), f32[128,8,128]{2,1,0:T(8,128)S(1)}, u32[]{:S(2)}, u32[]{:S(2)}) %all-to-all-start) | async-done | bytes 524320 | tf_op jit(solution)/shard_map/all_to_all | solution.py:315
  87.4 1.3 shard_map.46
  88.7 2.0 collective-permute-start
  90.6 1.5 collective-permute-done.got
  92.2 0.4 shard_map.47
  92.6 2.4 %collective-permute-start.1 = (f32[256,512]{1,0:T(8,128)S(1)}, f32[256,512]{1,0:T(8,128)S(1)}, u32[]{:S(2)}, u32[]{:S(2)}) collective-permute-start(f32[256,512]{1,0:T(8,128)S(1)} %get-tuple-element.94.refs_2_), channel_id=1, source_target_pairs={{1,3},{3,5},{5,7},{7,9},{9,11},{11,13},{13,15},{15,17},{17,19},{19... | collective-permute-start | bytes 1572872 | tf_op jit(solution)/shard_map/ppermute | solution.py:331
  95.0 2.6 %collective-permute-start.3 = (f32[256,512]{1,0:T(8,128)S(1)}, f32[256,512]{1,0:T(8,128)S(1)}, u32[]{:S(2)}, u32[]{:S(2)}) collective-permute-start(f32[256,512]{1,0:T(8,128)S(1)} %get-tuple-element.94.refs_2_), channel_id=1, source_target_pairs={{0,1},{1,0},{2,3},{3,2},{4,5},{5,4},{6,7},{7,6},{8,9},{9,8},{10,11... | collective-permute-start | bytes 1572872 | tf_op jit(solution)/shard_map/ppermute | solution.py:332
  97.6 2.0 collective-permute-start.5
  99.6 6.2 %collective-permute-done.1.refs_2_ = f32[256,512]{1,0:T(8,128)S(1)} collective-permute-done((f32[256,512]{1,0:T(8,128)S(1)}, f32[256,512]{1,0:T(8,128)S(1)}, u32[]{:S(2)}, u32[]{:S(2)}) %collective-permute-start.1) | collective-permute-done | bytes 524320 | tf_op jit(solution)/shard_map/ppermute | solution.py:331
  105.8 1.9 collective-permute-start.2
  107.8 2.1 %collective-permute-start.4 = (f32[224,512]{1,0:T(8,128)S(1)}, f32[224,512]{1,0:T(8,128)S(1)}, u32[]{:S(2)}, u32[]{:S(2)}) collective-permute-start(f32[224,512]{1,0:T(8,128)S(1)} %get-tuple-element.101), channel_id=1, source_target_pairs={{0,2},{2,4},{4,6},{6,8},{8,10},{10,12},{12,14},{14,16},{16,18},{18... | collective-permute-start | bytes 1376264 | tf_op jit(solution)/shard_map/ppermute | solution.py:333
  109.9 2.0 tables.6
  112.0 0.8 copy-done.5
  112.9 0.6 shard_map.48.refs_3_
  113.5 0.4 shard_map.49.refs_3_
  113.9 0.4 shard_map.50.part
  114.3 3.8 %collective-permute-done.4.second = f32[224,512]{1,0:T(8,128)S(1)} collective-permute-done((f32[224,512]{1,0:T(8,128)S(1)}, f32[224,512]{1,0:T(8,128)S(1)}, u32[]{:S(2)}, u32[]{:S(2)}) %collective-permute-start.4) | collective-permute-done | bytes 458784 | tf_op jit(solution)/shard_map/ppermute | solution.py:333
  118.2 1.3 shard_map.53
  119.5 2.0 collective-permute-start.6
  121.4 3.4 %collective-permute-start.8 = (f32[256,512]{1,0:T(8,128)S(1)}, f32[256,512]{1,0:T(8,128)S(1)}, u32[]{:S(2)}, u32[]{:S(2)}) collective-permute-start(f32[256,512]{1,0:T(8,128)S(1)} %get-tuple-element.110.refs_2_), channel_id=1, source_target_pairs={{0,1},{1,0},{2,3},{3,2},{4,5},{5,4},{6,7},{7,6},{8,9},{9,8},{10,11... | collective-permute-start | bytes 1572872 | tf_op jit(solution)/shard_map/ppermute | solution.py:332
  124.8 2.0 collective-permute-start.10
  126.8 5.9 %collective-permute-done.6.refs_2_ = f32[256,512]{1,0:T(8,128)S(1)} collective-permute-done((f32[256,512]{1,0:T(8,128)S(1)}, f32[256,512]{1,0:T(8,128)S(1)}, u32[]{:S(2)}, u32[]{:S(2)}) %collective-permute-start.6) | collective-permute-done | bytes 524320 | tf_op jit(solution)/shard_map/ppermute | solution.py:331
  132.7 1.9 collective-permute-start.7
  134.6 2.7 %collective-permute-start.9 = (f32[224,512]{1,0:T(8,128)S(1)}, f32[224,512]{1,0:T(8,128)S(1)}, u32[]{:S(2)}, u32[]{:S(2)}) collective-permute-start(f32[224,512]{1,0:T(8,128)S(1)} %get-tuple-element.117), channel_id=1, source_target_pairs={{0,2},{2,4},{4,6},{6,8},{8,10},{10,12},{12,14},{14,16},{16,18},{18... | collective-permute-start | bytes 1376264 | tf_op jit(solution)/shard_map/ppermute | solution.py:333
  137.3 2.0 tables.5
  139.4 0.6 shard_map.54.refs_3_
  140.0 0.4 shard_map.55.refs_3_
  140.5 0.4 shard_map.56.part
  140.9 4.2 %collective-permute-done.9.second = f32[224,512]{1,0:T(8,128)S(1)} collective-permute-done((f32[224,512]{1,0:T(8,128)S(1)}, f32[224,512]{1,0:T(8,128)S(1)}, u32[]{:S(2)}, u32[]{:S(2)}) %collective-permute-start.9) | collective-permute-done | bytes 458784 | tf_op jit(solution)/shard_map/ppermute | solution.py:333
  145.0 1.3 shard_map.58
  146.3 2.0 collective-permute-start.11
  148.2 3.4 %collective-permute-start.13 = (f32[256,512]{1,0:T(8,128)S(1)}, f32[256,512]{1,0:T(8,128)S(1)}, u32[]{:S(2)}, u32[]{:S(2)}) collective-permute-start(f32[256,512]{1,0:T(8,128)S(1)} %get-tuple-element.127.refs_2_), channel_id=1, source_target_pairs={{0,1},{1,0},{2,3},{3,2},{4,5},{5,4},{6,7},{7,6},{8,9},{9,8},{10,11... | collective-permute-start | bytes 1572872 | tf_op jit(solution)/shard_map/ppermute | solution.py:332
  151.7 7.8 %collective-permute-done.11.refs_2_ = f32[256,512]{1,0:T(8,128)S(1)} collective-permute-done((f32[256,512]{1,0:T(8,128)S(1)}, f32[256,512]{1,0:T(8,128)S(1)}, u32[]{:S(2)}, u32[]{:S(2)}) %collective-permute-start.11) | collective-permute-done | bytes 524320 | tf_op jit(solution)/shard_map/ppermute | solution.py:331
  159.5 1.9 collective-permute-start.12
  161.5 2.5 %collective-permute-start.14 = (f32[224,512]{1,0:T(8,128)S(1)}, f32[224,512]{1,0:T(8,128)S(1)}, u32[]{:S(2)}, u32[]{:S(2)}) collective-permute-start(f32[224,512]{1,0:T(8,128)S(1)} %get-tuple-element.134), channel_id=1, source_target_pairs={{0,2},{2,4},{4,6},{6,8},{8,10},{10,12},{12,14},{14,16},{16,18},{18... | collective-permute-start | bytes 1376264 | tf_op jit(solution)/shard_map/ppermute | solution.py:333
  164.0 2.0 tables.4
  166.0 0.6 shard_map.59.refs_3_
  166.6 0.4 shard_map.60.refs_3_
  167.0 0.4 shard_map.61.part
  167.4 4.5 %collective-permute-done.14.second = f32[224,512]{1,0:T(8,128)S(1)} collective-permute-done((f32[224,512]{1,0:T(8,128)S(1)}, f32[224,512]{1,0:T(8,128)S(1)}, u32[]{:S(2)}, u32[]{:S(2)}) %collective-permute-start.14) | collective-permute-done | bytes 458784 | tf_op jit(solution)/shard_map/ppermute | solution.py:333
  171.9 1.3 shard_map.62
  173.1 2.0 collective-permute-start.15
  175.1 3.4 %collective-permute-start.17 = (f32[256,512]{1,0:T(8,128)S(1)}, f32[256,512]{1,0:T(8,128)S(1)}, u32[]{:S(2)}, u32[]{:S(2)}) collective-permute-start(f32[256,512]{1,0:T(8,128)S(1)} %get-tuple-element.142.refs_2_), channel_id=1, source_target_pairs={{0,1},{1,0},{2,3},{3,2},{4,5},{5,4},{6,7},{7,6},{8,9},{9,8},{10,11... | collective-permute-start | bytes 1572872 | tf_op jit(solution)/shard_map/ppermute | solution.py:332
  178.5 7.8 %collective-permute-done.15.refs_2_ = f32[256,512]{1,0:T(8,128)S(1)} collective-permute-done((f32[256,512]{1,0:T(8,128)S(1)}, f32[256,512]{1,0:T(8,128)S(1)}, u32[]{:S(2)}, u32[]{:S(2)}) %collective-permute-start.15) | collective-permute-done | bytes 524320 | tf_op jit(solution)/shard_map/ppermute | solution.py:331
  186.3 1.9 collective-permute-start.16
  188.3 2.5 %collective-permute-start.18 = (f32[224,512]{1,0:T(8,128)S(1)}, f32[224,512]{1,0:T(8,128)S(1)}, u32[]{:S(2)}, u32[]{:S(2)}) collective-permute-start(f32[224,512]{1,0:T(8,128)S(1)} %get-tuple-element.149), channel_id=1, source_target_pairs={{0,2},{2,4},{4,6},{6,8},{8,10},{10,12},{12,14},{14,16},{16,18},{18... | collective-permute-start | bytes 1376264 | tf_op jit(solution)/shard_map/ppermute | solution.py:333
  190.9 0.6 shard_map.63.refs_3_
  191.5 0.4 shard_map.64.refs_3_
  191.9 0.4 shard_map.65.part
  192.3 6.4 %collective-permute-done.18.second = f32[224,512]{1,0:T(8,128)S(1)} collective-permute-done((f32[224,512]{1,0:T(8,128)S(1)}, f32[224,512]{1,0:T(8,128)S(1)}, u32[]{:S(2)}, u32[]{:S(2)}) %collective-permute-start.18) | collective-permute-done | bytes 458784 | tf_op jit(solution)/shard_map/ppermute | solution.py:333
  198.7 0.4 shard_map.66
  199.1 3.4 %collective-permute-start.19 = (f32[128,512]{1,0:T(8,128)S(1)}, f32[128,512]{1,0:T(8,128)S(1)}, u32[]{:S(2)}, u32[]{:S(2)}) collective-permute-start(f32[128,512]{1,0:T(8,128)S(1)} %get-tuple-element.154), channel_id=1, source_target_pairs={{0,1},{1,0},{2,3},{3,2},{4,5},{5,4},{6,7},{7,6},{8,9},{9,8},{10,11... | collective-permute-start | bytes 786440 | tf_op jit(solution)/shard_map/ppermute | solution.py:352
  202.5 1.1 collective-permute-done.19.got
  203.7 0.8 shard_map.67
  (34 shorter events, 0.5 us)
Async XLA Ops:
  0.0 1.0 copy-start
  2.3 85.0 %all-to-all-start = ((f32[128,8,128]{2,1,0:T(8,128)}), f32[128,8,128]{2,1,0:T(8,128)S(1)}, u32[]{:S(2)}, u32[]{:S(2)}) async-start(f32[128,8,128]{2,1,0:T(8,128)} %bitcast.2), calls=%async_computation | async-start | bytes 1048576 | tf_op jit(solution)/shard_map/all_to_all | solution.py:315
  53.8 33.6 %copy-start.1 = (f32[16,16,512]{2,1,0:T(8,128)S(1)}, f32[16,16,512]{2,1,0:T(8,128)}, u32[]{:S(2)}) copy-start(f32[16,16,512]{2,1,0:T(8,128)} %param.4) | copy-start | bytes 1572868
  53.8 0.7 copy-start.2
  56.5 0.7 copy-start.4
  57.1 0.7 copy-start.6
  57.8 0.6 copy-start.8
  58.4 0.7 copy-start.10
  59.1 0.6 copy-start.12
  87.4 4.8 %copy-start.11 = (bf16[256,256]{1,0:T(8,128)(2,1)S(1)}, bf16[256,256]{1,0:T(8,128)(2,1)}, u32[]{:S(2)}) copy-start(bf16[256,256]{1,0:T(8,128)(2,1)} %copy-done.10) | copy-start | bytes 393220
  87.4 4.8 %copy-start.13 = (bf16[256,256]{1,0:T(8,128)(2,1)S(1)}, bf16[256,256]{1,0:T(8,128)(2,1)}, u32[]{:S(2)}) copy-start(bf16[256,256]{1,0:T(8,128)(2,1)} %copy-done.12) | copy-start | bytes 393220
  88.7 3.5 %collective-permute-start = (f32[128,512]{1,0:T(8,128)S(1)}, f32[128,512]{1,0:T(8,128)S(1)}, u32[]{:S(2)}, u32[]{:S(2)}) collective-permute-start(f32[128,512]{1,0:T(8,128)S(1)} %get-tuple-element.91), channel_id=1, source_target_pairs={{0,1},{1,0},{2,3},{3,2},{4,5},{5,4},{6,7},{7,6},{8,9},{9,8},{10,11... | collective-permute-start | bytes 786440 | tf_op jit(solution)/shard_map/ppermute | solution.py:327
  92.6 13.2 %collective-permute-start.1 = (f32[256,512]{1,0:T(8,128)S(1)}, f32[256,512]{1,0:T(8,128)S(1)}, u32[]{:S(2)}, u32[]{:S(2)}) collective-permute-start(f32[256,512]{1,0:T(8,128)S(1)} %get-tuple-element.94.refs_2_), channel_id=1, source_target_pairs={{1,3},{3,5},{5,7},{7,9},{9,11},{11,13},{13,15},{15,17},{17,19},{19... | collective-permute-start | bytes 1572872 | tf_op jit(solution)/shard_map/ppermute | solution.py:331
  95.0 17.0 %collective-permute-start.3 = (f32[256,512]{1,0:T(8,128)S(1)}, f32[256,512]{1,0:T(8,128)S(1)}, u32[]{:S(2)}, u32[]{:S(2)}) collective-permute-start(f32[256,512]{1,0:T(8,128)S(1)} %get-tuple-element.94.refs_2_), channel_id=1, source_target_pairs={{0,1},{1,0},{2,3},{3,2},{4,5},{5,4},{6,7},{7,6},{8,9},{9,8},{10,11... | collective-permute-start | bytes 1572872 | tf_op jit(solution)/shard_map/ppermute | solution.py:332
  97.6 14.2 %collective-permute-start.5 = (f32[128,512]{1,0:T(8,128)S(1)}, f32[128,512]{1,0:T(8,128)S(1)}, u32[]{:S(2)}, u32[]{:S(2)}) collective-permute-start(f32[128,512]{1,0:T(8,128)S(1)} %get-tuple-element.105), channel_id=1, source_target_pairs={{0,1},{1,0},{2,3},{3,2},{4,5},{5,4},{6,7},{7,6},{8,9},{9,8},{10,11... | collective-permute-start | bytes 786440 | tf_op jit(solution)/shard_map/ppermute | solution.py:318
  105.8 8.1 %collective-permute-start.2 = (f32[256,512]{1,0:T(8,128)S(1)}, f32[256,512]{1,0:T(8,128)S(1)}, u32[]{:S(2)}, u32[]{:S(2)}) collective-permute-start(f32[256,512]{1,0:T(8,128)S(1)} %collective-permute-done.1.refs_2_), channel_id=1, source_target_pairs={{0,1},{1,0},{2,3},{3,2},{4,5},{5,4},{6,7},{7,6},{8,9},{9,8},{10,11... | collective-permute-start | bytes 1572872 | tf_op jit(solution)/shard_map/ppermute | solution.py:337
  107.8 10.4 %collective-permute-start.4 = (f32[224,512]{1,0:T(8,128)S(1)}, f32[224,512]{1,0:T(8,128)S(1)}, u32[]{:S(2)}, u32[]{:S(2)}) collective-permute-start(f32[224,512]{1,0:T(8,128)S(1)} %get-tuple-element.101), channel_id=1, source_target_pairs={{0,2},{2,4},{4,6},{6,8},{8,10},{10,12},{12,14},{14,16},{16,18},{18... | collective-permute-start | bytes 1376264 | tf_op jit(solution)/shard_map/ppermute | solution.py:333
  111.9 0.9 copy-start.5
  111.9 1.0 copy-start.7
  111.9 1.0 copy-start.9
  119.4 17.9 %copy-start.3 = (f32[3,31]{1,0:T(4,128)S(1)}, f32[3,31]{1,0:T(4,128)}, u32[]{:S(2)}) copy-start(f32[3,31]{1,0:T(4,128)} %spread_ref.5) | copy-start | bytes 1120
  119.5 13.2 %collective-permute-start.6 = (f32[256,512]{1,0:T(8,128)S(1)}, f32[256,512]{1,0:T(8,128)S(1)}, u32[]{:S(2)}, u32[]{:S(2)}) collective-permute-start(f32[256,512]{1,0:T(8,128)S(1)} %get-tuple-element.110.refs_2_), channel_id=1, source_target_pairs={{1,3},{3,5},{5,7},{7,9},{9,11},{11,13},{13,15},{15,17},{17,19},{19... | collective-permute-start | bytes 1572872 | tf_op jit(solution)/shard_map/ppermute | solution.py:331
  121.4 18.0 %collective-permute-start.8 = (f32[256,512]{1,0:T(8,128)S(1)}, f32[256,512]{1,0:T(8,128)S(1)}, u32[]{:S(2)}, u32[]{:S(2)}) collective-permute-start(f32[256,512]{1,0:T(8,128)S(1)} %get-tuple-element.110.refs_2_), channel_id=1, source_target_pairs={{0,1},{1,0},{2,3},{3,2},{4,5},{5,4},{6,7},{7,6},{8,9},{9,8},{10,11... | collective-permute-start | bytes 1572872 | tf_op jit(solution)/shard_map/ppermute | solution.py:332
  124.8 14.5 %collective-permute-start.10 = (f32[128,512]{1,0:T(8,128)S(1)}, f32[128,512]{1,0:T(8,128)S(1)}, u32[]{:S(2)}, u32[]{:S(2)}) collective-permute-start(f32[128,512]{1,0:T(8,128)S(1)} %get-tuple-element.121), channel_id=1, source_target_pairs={{0,1},{1,0},{2,3},{3,2},{4,5},{5,4},{6,7},{7,6},{8,9},{9,8},{10,11... | collective-permute-start | bytes 786440 | tf_op jit(solution)/shard_map/ppermute | solution.py:340
  132.7 7.8 %collective-permute-start.7 = (f32[256,512]{1,0:T(8,128)S(1)}, f32[256,512]{1,0:T(8,128)S(1)}, u32[]{:S(2)}, u32[]{:S(2)}) collective-permute-start(f32[256,512]{1,0:T(8,128)S(1)} %collective-permute-done.6.refs_2_), channel_id=1, source_target_pairs={{0,1},{1,0},{2,3},{3,2},{4,5},{5,4},{6,7},{7,6},{8,9},{9,8},{10,11... | collective-permute-start | bytes 1572872 | tf_op jit(solution)/shard_map/ppermute | solution.py:337
  134.6 10.4 %collective-permute-start.9 = (f32[224,512]{1,0:T(8,128)S(1)}, f32[224,512]{1,0:T(8,128)S(1)}, u32[]{:S(2)}, u32[]{:S(2)}) collective-permute-start(f32[224,512]{1,0:T(8,128)S(1)} %get-tuple-element.117), channel_id=1, source_target_pairs={{0,2},{2,4},{4,6},{6,8},{8,10},{10,12},{12,14},{14,16},{16,18},{18... | collective-permute-start | bytes 1376264 | tf_op jit(solution)/shard_map/ppermute | solution.py:333
  146.3 13.2 %collective-permute-start.11 = (f32[256,512]{1,0:T(8,128)S(1)}, f32[256,512]{1,0:T(8,128)S(1)}, u32[]{:S(2)}, u32[]{:S(2)}) collective-permute-start(f32[256,512]{1,0:T(8,128)S(1)} %get-tuple-element.127.refs_2_), channel_id=1, source_target_pairs={{1,3},{3,5},{5,7},{7,9},{9,11},{11,13},{13,15},{15,17},{17,19},{19... | collective-permute-start | bytes 1572872 | tf_op jit(solution)/shard_map/ppermute | solution.py:331
  148.2 17.7 %collective-permute-start.13 = (f32[256,512]{1,0:T(8,128)S(1)}, f32[256,512]{1,0:T(8,128)S(1)}, u32[]{:S(2)}, u32[]{:S(2)}) collective-permute-start(f32[256,512]{1,0:T(8,128)S(1)} %get-tuple-element.127.refs_2_), channel_id=1, source_target_pairs={{0,1},{1,0},{2,3},{3,2},{4,5},{5,4},{6,7},{7,6},{8,9},{9,8},{10,11... | collective-permute-start | bytes 1572872 | tf_op jit(solution)/shard_map/ppermute | solution.py:332
  159.5 7.5 %collective-permute-start.12 = (f32[256,512]{1,0:T(8,128)S(1)}, f32[256,512]{1,0:T(8,128)S(1)}, u32[]{:S(2)}, u32[]{:S(2)}) collective-permute-start(f32[256,512]{1,0:T(8,128)S(1)} %collective-permute-done.11.refs_2_), channel_id=1, source_target_pairs={{0,1},{1,0},{2,3},{3,2},{4,5},{5,4},{6,7},{7,6},{8,9},{9,8},{10,11... | collective-permute-start | bytes 1572872 | tf_op jit(solution)/shard_map/ppermute | solution.py:337
  161.5 10.4 %collective-permute-start.14 = (f32[224,512]{1,0:T(8,128)S(1)}, f32[224,512]{1,0:T(8,128)S(1)}, u32[]{:S(2)}, u32[]{:S(2)}) collective-permute-start(f32[224,512]{1,0:T(8,128)S(1)} %get-tuple-element.134), channel_id=1, source_target_pairs={{0,2},{2,4},{4,6},{6,8},{8,10},{10,12},{12,14},{14,16},{16,18},{18... | collective-permute-start | bytes 1376264 | tf_op jit(solution)/shard_map/ppermute | solution.py:333
  173.1 13.2 %collective-permute-start.15 = (f32[256,512]{1,0:T(8,128)S(1)}, f32[256,512]{1,0:T(8,128)S(1)}, u32[]{:S(2)}, u32[]{:S(2)}) collective-permute-start(f32[256,512]{1,0:T(8,128)S(1)} %get-tuple-element.142.refs_2_), channel_id=1, source_target_pairs={{1,3},{3,5},{5,7},{7,9},{9,11},{11,13},{13,15},{15,17},{17,19},{19... | collective-permute-start | bytes 1572872 | tf_op jit(solution)/shard_map/ppermute | solution.py:331
  175.1 15.8 %collective-permute-start.17 = (f32[256,512]{1,0:T(8,128)S(1)}, f32[256,512]{1,0:T(8,128)S(1)}, u32[]{:S(2)}, u32[]{:S(2)}) collective-permute-start(f32[256,512]{1,0:T(8,128)S(1)} %get-tuple-element.142.refs_2_), channel_id=1, source_target_pairs={{0,1},{1,0},{2,3},{3,2},{4,5},{5,4},{6,7},{7,6},{8,9},{9,8},{10,11... | collective-permute-start | bytes 1572872 | tf_op jit(solution)/shard_map/ppermute | solution.py:332
  186.3 5.5 %collective-permute-start.16 = (f32[256,512]{1,0:T(8,128)S(1)}, f32[256,512]{1,0:T(8,128)S(1)}, u32[]{:S(2)}, u32[]{:S(2)}) collective-permute-start(f32[256,512]{1,0:T(8,128)S(1)} %collective-permute-done.15.refs_2_), channel_id=1, source_target_pairs={{0,1},{1,0},{2,3},{3,2},{4,5},{5,4},{6,7},{7,6},{8,9},{9,8},{10,11... | collective-permute-start | bytes 1572872 | tf_op jit(solution)/shard_map/ppermute | solution.py:337
  188.3 10.4 %collective-permute-start.18 = (f32[224,512]{1,0:T(8,128)S(1)}, f32[224,512]{1,0:T(8,128)S(1)}, u32[]{:S(2)}, u32[]{:S(2)}) collective-permute-start(f32[224,512]{1,0:T(8,128)S(1)} %get-tuple-element.149), channel_id=1, source_target_pairs={{0,2},{2,4},{4,6},{6,8},{8,10},{10,12},{12,14},{14,16},{16,18},{18... | collective-permute-start | bytes 1376264 | tf_op jit(solution)/shard_map/ppermute | solution.py:333
  199.1 4.5 %collective-permute-start.19 = (f32[128,512]{1,0:T(8,128)S(1)}, f32[128,512]{1,0:T(8,128)S(1)}, u32[]{:S(2)}, u32[]{:S(2)}) collective-permute-start(f32[128,512]{1,0:T(8,128)S(1)} %get-tuple-element.154), channel_id=1, source_target_pairs={{0,1},{1,0},{2,3},{3,2},{4,5},{5,4},{6,7},{7,6},{8,9},{9,8},{10,11... | collective-permute-start | bytes 786440 | tf_op jit(solution)/shard_map/ppermute | solution.py:352

commit v4 on v3

--- a/solution.py
+++ b/solution.py
@@ -194,7 +194,7 @@
     )(*scalars, *operands)
 
 
-def start_kernel(planes, per_slab, core, messages, view, order, xh, xl, kept, given, kept_x, given_x, gathered, whole):
+def start_kernel(planes, per_slab, core, messages, view, order, xh, xl, kept, kept_x, given, gathered, whole):
     half = planes // 2
     rows = view.shape[0] // planes
     slabs = messages.shape[0] // half
@@ -212,10 +212,11 @@
     low = (rest - middle.astype(F32)).astype(BF16)
     dot = functools.partial(jnp.dot, preferred_element_type=F32)
     moved = (dot(high, order[...]) + dot(middle, order[...])) + dot(low, order[...])
+    count = kept.shape[0]
     whole[...] = moved
-    parted(core, whole, kept, given)
+    parted(core, whole, kept, given.at[count:])
     whole[...] = product(halves(0.5 * (view[...] + moved)), (xh[...], xl[...]))
-    parted(core, whole, kept_x, given_x)
+    parted(core, whole, kept_x, given.at[:count])
 
 
 def part_kernel(core, values, keep, give):
@@ -227,7 +228,7 @@
 
 
 def join_both_kernel(core, keep, got, view, values, estimate):
-    joined(core, keep, got, values)
+    joined(core, keep, got.at[keep.shape[0]:], values)
     estimate[...] = 0.5 * (view[...] + values[...])
 
 
@@ -242,7 +243,7 @@
 
 
 def enter_kernel(core, keep, got, yh, yl, whole, second, values):
-    joined(core, keep, got, values)
+    joined(core, keep, got.at[:keep.shape[0]], values)
     send_y(core, values[...], yh, yl, whole, second)
 
 
@@ -320,12 +321,12 @@
     table = table_of(0)
     order = ordering(count_x, per_slab)
 
-    kept, given, kept_x, given_x = call(
+    kept, kept_x, given = call(
         functools.partial(start_kernel, planes, per_slab), [core],
-        [arrived, first_y, order, *table[0:2]], [piece] * 4, [block, block],
+        [arrived, first_y, order, *table[0:2]], [piece, piece, block], [block, block],
     )
-    got_x = lax.ppermute(given_x, "gy", swap)
-    whole, ends_of = call(enter_kernel, [core], [kept_x, got_x, *table[2:4]], [block, ends], [block])
+    got = lax.ppermute(given, "gy", swap)
+    whole, ends_of = call(enter_kernel, [core], [kept_x, got, *table[2:4]], [block, ends], [block])
 
     for step in range(4):
         first_planes = lax.ppermute(whole, ("gz", "gy"), up[1] + down[0])
@@ -337,8 +338,7 @@
         forward_planes = lax.ppermute(first_planes, "gy", swap)
         part = partial([(*table[8:10], first_planes)], [part])
         if step == 0:
-            got_b = lax.ppermute(given, "gy", swap)
-            second, estimate = call(join_both_kernel, [core], [kept, got_b, first], [block, block])
+            second, estimate = call(join_both_kernel, [core], [kept, got, first], [block, block])
         part = partial([(*table[10:12], forward_planes)], [part])
         arrivals = (core, part, second_planes, table)
         if step % 2 == 0:

time: 206 us -> 206 us (level)
  waiting for transfers between devices: 77 us -> 79.4 us
  transfers between devices with their start and end apart: 21 -> 20, of which waited for: 11 -> 11; matrix products, arithmetic and copies ran while one was open for 0% -> 0% of each run, Pallas kernels for 7% -> 7%
where the time goes in v4:
time: 206 us; the launch traced here: 205 us
  starting transfers between devices  97.4 us (47%)
  waiting for transfers between devices  79.4 us (39%)
  Pallas kernels  21.7 us (11%)
  local copies, waits for them, and re-layouts  5.84 us (3%)
    all_to_all x1, starting transfers between devices, shards(): lax.all_to_all(packed.reshape(slabs, -1, lanes), 'gz', 0, 0, tiled=True)  51.4 us
    ppermute x4, waiting for transfers between devices, shards(): first_planes = lax.ppermute(whole, ('gz', 'gy'), up[1] + down[0])  29.8 us
    all_to_all x1, waiting for transfers between devices, shards(): lax.all_to_all(packed.reshape(slabs, -1, lanes), 'gz', 0, 0, tiled=True)  27.6 us
    ppermute x4, waiting for transfers between devices, shards(): second_planes = lax.ppermute(ends_of, ('gz', 'gy'), up[0] + down[1])  19 us
    ppermute x4, starting transfers between devices, shards(): side_planes = lax.ppermute(whole, 'gy', swap)  12.8 us
    pallas_call x22, Pallas kernels, call(): pl.pallas_call(kernel, out_shape=[jax.ShapeDtypeStruct(shape, F32) for sh...  12.5 us
    ppermute x4, starting transfers between devices, shards(): second_planes = lax.ppermute(ends_of, ('gz', 'gy'), up[0] + down[1])  9.89 us
    ppermute x4, starting transfers between devices, shards(): first_planes = lax.ppermute(whole, ('gz', 'gy'), up[1] + down[0])  8.23 us
  transfers between devices with their start and end apart: 20, of which 11 were waited for; matrix products, arithmetic and copies ran while one was open for 0% of the time, Pallas kernels for 7%

profile of v4, /device:TPU:94, one launch (start us, length us, event | category | flops | bytes accessed | tf_op | source)
XLA Modules:
  0.0 204.9 jit_solution(531483782857781589)
XLA Ops:
  0.0 1.0 copy-done
  1.0 1.3 pack.1
  2.3 51.4 %all-to-all-start = ((f32[128,8,128]{2,1,0:T(8,128)}), f32[128,8,128]{2,1,0:T(8,128)S(1)}, u32[]{:S(2)}, u32[]{:S(2)}) async-start(f32[128,8,128]{2,1,0:T(8,128)} %bitcast.2), calls=%async_computation | async-start | bytes 1048576 | tf_op jit(solution)/shard_map/all_to_all | solution.py:316
  53.8 0.1 ordering.1.order
  53.9 0.6 copy-done.2
  54.5 1.9 tables.7
  56.5 0.6 copy-done.4
  57.1 0.7 copy-done.6
  57.8 0.6 copy-done.8
  58.4 0.7 copy-done.10
  59.1 0.6 copy-done.12
  59.7 27.6 %all-to-all-done = f32[128,8,128]{2,1,0:T(8,128)S(1)} async-done(((f32[128,8,128]{2,1,0:T(8,128)}), f32[128,8,128]{2,1,0:T(8,128)S(1)}, u32[]{:S(2)}, u32[]{:S(2)}) %all-to-all-start) | async-done | bytes 524320 | tf_op jit(solution)/shard_map/all_to_all | solution.py:316
  87.4 1.3 shard_map.46
  88.7 2.0 collective-permute-start
  90.6 1.9 collective-permute-done.got
  92.5 0.4 shard_map.47
  93.0 2.4 %collective-permute-start.1 = (f32[256,512]{1,0:T(8,128)S(1)}, f32[256,512]{1,0:T(8,128)S(1)}, u32[]{:S(2)}, u32[]{:S(2)}) collective-permute-start(f32[256,512]{1,0:T(8,128)S(1)} %get-tuple-element.93.refs_2_), channel_id=1, source_target_pairs={{1,3},{3,5},{5,7},{7,9},{9,11},{11,13},{13,15},{15,17},{17,19},{19... | collective-permute-start | bytes 1572872 | tf_op jit(solution)/shard_map/ppermute | solution.py:332
  95.4 2.6 %collective-permute-start.3 = (f32[256,512]{1,0:T(8,128)S(1)}, f32[256,512]{1,0:T(8,128)S(1)}, u32[]{:S(2)}, u32[]{:S(2)}) collective-permute-start(f32[256,512]{1,0:T(8,128)S(1)} %get-tuple-element.93.refs_2_), channel_id=1, source_target_pairs={{0,1},{1,0},{2,3},{3,2},{4,5},{5,4},{6,7},{7,6},{8,9},{9,8},{10,11... | collective-permute-start | bytes 1572872 | tf_op jit(solution)/shard_map/ppermute | solution.py:333
  98.0 2.0 collective-permute-start.5
  100.0 6.2 %collective-permute-done.1.refs_2_ = f32[256,512]{1,0:T(8,128)S(1)} collective-permute-done((f32[256,512]{1,0:T(8,128)S(1)}, f32[256,512]{1,0:T(8,128)S(1)}, u32[]{:S(2)}, u32[]{:S(2)}) %collective-permute-start.1) | collective-permute-done | bytes 524320 | tf_op jit(solution)/shard_map/ppermute | solution.py:332
  106.2 1.9 collective-permute-start.2
  108.1 2.1 %collective-permute-start.4 = (f32[224,512]{1,0:T(8,128)S(1)}, f32[224,512]{1,0:T(8,128)S(1)}, u32[]{:S(2)}, u32[]{:S(2)}) collective-permute-start(f32[224,512]{1,0:T(8,128)S(1)} %get-tuple-element.100), channel_id=1, source_target_pairs={{0,2},{2,4},{4,6},{6,8},{8,10},{10,12},{12,14},{14,16},{16,18},{18... | collective-permute-start | bytes 1376264 | tf_op jit(solution)/shard_map/ppermute | solution.py:334
  110.3 2.0 tables.6
  112.3 0.8 copy-done.5
  113.3 0.6 shard_map.48.refs_3_
  113.9 0.4 shard_map.49.refs_3_
  114.3 0.4 shard_map.50.part
  114.7 3.8 %collective-permute-done.4.second = f32[224,512]{1,0:T(8,128)S(1)} collective-permute-done((f32[224,512]{1,0:T(8,128)S(1)}, f32[224,512]{1,0:T(8,128)S(1)}, u32[]{:S(2)}, u32[]{:S(2)}) %collective-permute-start.4) | collective-permute-done | bytes 458784 | tf_op jit(solution)/shard_map/ppermute | solution.py:334
  118.5 1.3 shard_map.53
  119.8 2.0 collective-permute-start.6
  121.8 3.4 %collective-permute-start.8 = (f32[256,512]{1,0:T(8,128)S(1)}, f32[256,512]{1,0:T(8,128)S(1)}, u32[]{:S(2)}, u32[]{:S(2)}) collective-permute-start(f32[256,512]{1,0:T(8,128)S(1)} %get-tuple-element.109.refs_2_), channel_id=1, source_target_pairs={{0,1},{1,0},{2,3},{3,2},{4,5},{5,4},{6,7},{7,6},{8,9},{9,8},{10,11... | collective-permute-start | bytes 1572872 | tf_op jit(solution)/shard_map/ppermute | solution.py:333
  125.2 7.9 %collective-permute-done.6.refs_2_ = f32[256,512]{1,0:T(8,128)S(1)} collective-permute-done((f32[256,512]{1,0:T(8,128)S(1)}, f32[256,512]{1,0:T(8,128)S(1)}, u32[]{:S(2)}, u32[]{:S(2)}) %collective-permute-start.6) | collective-permute-done | bytes 524320 | tf_op jit(solution)/shard_map/ppermute | solution.py:332
  133.0 1.9 collective-permute-start.7
  135.0 2.7 %collective-permute-start.9 = (f32[224,512]{1,0:T(8,128)S(1)}, f32[224,512]{1,0:T(8,128)S(1)}, u32[]{:S(2)}, u32[]{:S(2)}) collective-permute-start(f32[224,512]{1,0:T(8,128)S(1)} %get-tuple-element.116), channel_id=1, source_target_pairs={{0,2},{2,4},{4,6},{6,8},{8,10},{10,12},{12,14},{14,16},{16,18},{18... | collective-permute-start | bytes 1376264 | tf_op jit(solution)/shard_map/ppermute | solution.py:334
  137.7 2.0 tables.5
  139.8 0.6 shard_map.54.refs_3_
  140.4 0.4 shard_map.55.refs_3_
  140.8 0.4 shard_map.56.part
  141.2 4.2 %collective-permute-done.9.second = f32[224,512]{1,0:T(8,128)S(1)} collective-permute-done((f32[224,512]{1,0:T(8,128)S(1)}, f32[224,512]{1,0:T(8,128)S(1)}, u32[]{:S(2)}, u32[]{:S(2)}) %collective-permute-start.9) | collective-permute-done | bytes 458784 | tf_op jit(solution)/shard_map/ppermute | solution.py:334
  145.4 1.3 shard_map.58
  146.7 2.0 collective-permute-start.10
  148.6 3.4 %collective-permute-start.12 = (f32[256,512]{1,0:T(8,128)S(1)}, f32[256,512]{1,0:T(8,128)S(1)}, u32[]{:S(2)}, u32[]{:S(2)}) collective-permute-start(f32[256,512]{1,0:T(8,128)S(1)} %get-tuple-element.125.refs_2_), channel_id=1, source_target_pairs={{0,1},{1,0},{2,3},{3,2},{4,5},{5,4},{6,7},{7,6},{8,9},{9,8},{10,11... | collective-permute-start | bytes 1572872 | tf_op jit(solution)/shard_map/ppermute | solution.py:333
  152.0 7.9 %collective-permute-done.10.refs_2_ = f32[256,512]{1,0:T(8,128)S(1)} collective-permute-done((f32[256,512]{1,0:T(8,128)S(1)}, f32[256,512]{1,0:T(8,128)S(1)}, u32[]{:S(2)}, u32[]{:S(2)}) %collective-permute-start.10) | collective-permute-done | bytes 524320 | tf_op jit(solution)/shard_map/ppermute | solution.py:332
  159.9 1.9 collective-permute-start.11
  161.8 2.5 %collective-permute-start.13 = (f32[224,512]{1,0:T(8,128)S(1)}, f32[224,512]{1,0:T(8,128)S(1)}, u32[]{:S(2)}, u32[]{:S(2)}) collective-permute-start(f32[224,512]{1,0:T(8,128)S(1)} %get-tuple-element.132), channel_id=1, source_target_pairs={{0,2},{2,4},{4,6},{6,8},{8,10},{10,12},{12,14},{14,16},{16,18},{18... | collective-permute-start | bytes 1376264 | tf_op jit(solution)/shard_map/ppermute | solution.py:334
  164.4 2.0 tables.4
  166.3 0.6 shard_map.59.refs_3_
  166.9 0.4 shard_map.60.refs_3_
  167.3 0.4 shard_map.61.part
  167.7 4.5 %collective-permute-done.13.second = f32[224,512]{1,0:T(8,128)S(1)} collective-permute-done((f32[224,512]{1,0:T(8,128)S(1)}, f32[224,512]{1,0:T(8,128)S(1)}, u32[]{:S(2)}, u32[]{:S(2)}) %collective-permute-start.13) | collective-permute-done | bytes 458784 | tf_op jit(solution)/shard_map/ppermute | solution.py:334
  172.2 1.3 shard_map.62
  173.5 2.0 collective-permute-start.14
  175.5 3.4 %collective-permute-start.16 = (f32[256,512]{1,0:T(8,128)S(1)}, f32[256,512]{1,0:T(8,128)S(1)}, u32[]{:S(2)}, u32[]{:S(2)}) collective-permute-start(f32[256,512]{1,0:T(8,128)S(1)} %get-tuple-element.140.refs_2_), channel_id=1, source_target_pairs={{0,1},{1,0},{2,3},{3,2},{4,5},{5,4},{6,7},{7,6},{8,9},{9,8},{10,11... | collective-permute-start | bytes 1572872 | tf_op jit(solution)/shard_map/ppermute | solution.py:333
  178.9 7.9 %collective-permute-done.14.refs_2_ = f32[256,512]{1,0:T(8,128)S(1)} collective-permute-done((f32[256,512]{1,0:T(8,128)S(1)}, f32[256,512]{1,0:T(8,128)S(1)}, u32[]{:S(2)}, u32[]{:S(2)}) %collective-permute-start.14) | collective-permute-done | bytes 524320 | tf_op jit(solution)/shard_map/ppermute | solution.py:332
  186.7 1.9 collective-permute-start.15
  188.7 2.5 %collective-permute-start.17 = (f32[224,512]{1,0:T(8,128)S(1)}, f32[224,512]{1,0:T(8,128)S(1)}, u32[]{:S(2)}, u32[]{:S(2)}) collective-permute-start(f32[224,512]{1,0:T(8,128)S(1)} %get-tuple-element.147), channel_id=1, source_target_pairs={{0,2},{2,4},{4,6},{6,8},{8,10},{10,12},{12,14},{14,16},{16,18},{18... | collective-permute-start | bytes 1376264 | tf_op jit(solution)/shard_map/ppermute | solution.py:334
  191.2 0.6 shard_map.63.refs_3_
  191.8 0.4 shard_map.64.refs_3_
  192.2 0.4 shard_map.65.part
  192.6 6.4 %collective-permute-done.17.second = f32[224,512]{1,0:T(8,128)S(1)} collective-permute-done((f32[224,512]{1,0:T(8,128)S(1)}, f32[224,512]{1,0:T(8,128)S(1)}, u32[]{:S(2)}, u32[]{:S(2)}) %collective-permute-start.17) | collective-permute-done | bytes 458784 | tf_op jit(solution)/shard_map/ppermute | solution.py:334
  199.1 0.4 shard_map.66
  199.5 3.4 %collective-permute-start.18 = (f32[128,512]{1,0:T(8,128)S(1)}, f32[128,512]{1,0:T(8,128)S(1)}, u32[]{:S(2)}, u32[]{:S(2)}) collective-permute-start(f32[128,512]{1,0:T(8,128)S(1)} %get-tuple-element.152), channel_id=1, source_target_pairs={{0,1},{1,0},{2,3},{3,2},{4,5},{5,4},{6,7},{7,6},{8,9},{9,8},{10,11... | collective-permute-start | bytes 786440 | tf_op jit(solution)/shard_map/ppermute | solution.py:352
  202.9 1.1 collective-permute-done.18.got
  204.0 0.8 shard_map.67
  (32 shorter events, 0.4 us)
Async XLA Ops:
  0.0 1.0 copy-start
  2.3 85.0 %all-to-all-start = ((f32[128,8,128]{2,1,0:T(8,128)}), f32[128,8,128]{2,1,0:T(8,128)S(1)}, u32[]{:S(2)}, u32[]{:S(2)}) async-start(f32[128,8,128]{2,1,0:T(8,128)} %bitcast.2), calls=%async_computation | async-start | bytes 1048576 | tf_op jit(solution)/shard_map/all_to_all | solution.py:316
  53.8 33.6 %copy-start.1 = (f32[16,16,512]{2,1,0:T(8,128)S(1)}, f32[16,16,512]{2,1,0:T(8,128)}, u32[]{:S(2)}) copy-start(f32[16,16,512]{2,1,0:T(8,128)} %param.4) | copy-start | bytes 1572868
  53.8 0.7 copy-start.2
  56.5 0.7 copy-start.4
  57.1 0.7 copy-start.6
  57.8 0.6 copy-start.8
  58.4 0.7 copy-start.10
  59.1 0.7 copy-start.12
  87.4 5.2 %copy-start.11 = (bf16[256,256]{1,0:T(8,128)(2,1)S(1)}, bf16[256,256]{1,0:T(8,128)(2,1)}, u32[]{:S(2)}) copy-start(bf16[256,256]{1,0:T(8,128)(2,1)} %copy-done.10) | copy-start | bytes 393220
  87.4 5.2 %copy-start.13 = (bf16[256,256]{1,0:T(8,128)(2,1)S(1)}, bf16[256,256]{1,0:T(8,128)(2,1)}, u32[]{:S(2)}) copy-start(bf16[256,256]{1,0:T(8,128)(2,1)} %copy-done.12) | copy-start | bytes 393220
  88.7 3.8 %collective-permute-start = (f32[256,512]{1,0:T(8,128)S(1)}, f32[256,512]{1,0:T(8,128)S(1)}, u32[]{:S(2)}, u32[]{:S(2)}) collective-permute-start(f32[256,512]{1,0:T(8,128)S(1)} %get-tuple-element.90), channel_id=1, source_target_pairs={{0,1},{1,0},{2,3},{3,2},{4,5},{5,4},{6,7},{7,6},{8,9},{9,8},{10,11... | collective-permute-start | bytes 1572872 | tf_op jit(solution)/shard_map/ppermute | solution.py:328
  93.0 13.2 %collective-permute-start.1 = (f32[256,512]{1,0:T(8,128)S(1)}, f32[256,512]{1,0:T(8,128)S(1)}, u32[]{:S(2)}, u32[]{:S(2)}) collective-permute-start(f32[256,512]{1,0:T(8,128)S(1)} %get-tuple-element.93.refs_2_), channel_id=1, source_target_pairs={{1,3},{3,5},{5,7},{7,9},{9,11},{11,13},{13,15},{15,17},{17,19},{19... | collective-permute-start | bytes 1572872 | tf_op jit(solution)/shard_map/ppermute | solution.py:332
  95.4 17.0 %collective-permute-start.3 = (f32[256,512]{1,0:T(8,128)S(1)}, f32[256,512]{1,0:T(8,128)S(1)}, u32[]{:S(2)}, u32[]{:S(2)}) collective-permute-start(f32[256,512]{1,0:T(8,128)S(1)} %get-tuple-element.93.refs_2_), channel_id=1, source_target_pairs={{0,1},{1,0},{2,3},{3,2},{4,5},{5,4},{6,7},{7,6},{8,9},{9,8},{10,11... | collective-permute-start | bytes 1572872 | tf_op jit(solution)/shard_map/ppermute | solution.py:333
  98.0 14.2 %collective-permute-start.5 = (f32[128,512]{1,0:T(8,128)S(1)}, f32[128,512]{1,0:T(8,128)S(1)}, u32[]{:S(2)}, u32[]{:S(2)}) collective-permute-start(f32[128,512]{1,0:T(8,128)S(1)} %get-tuple-element.104), channel_id=1, source_target_pairs={{0,1},{1,0},{2,3},{3,2},{4,5},{5,4},{6,7},{7,6},{8,9},{9,8},{10,11... | collective-permute-start | bytes 786440 | tf_op jit(solution)/shard_map/ppermute | solution.py:319
  106.2 8.1 %collective-permute-start.2 = (f32[256,512]{1,0:T(8,128)S(1)}, f32[256,512]{1,0:T(8,128)S(1)}, u32[]{:S(2)}, u32[]{:S(2)}) collective-permute-start(f32[256,512]{1,0:T(8,128)S(1)} %collective-permute-done.1.refs_2_), channel_id=1, source_target_pairs={{0,1},{1,0},{2,3},{3,2},{4,5},{5,4},{6,7},{7,6},{8,9},{9,8},{10,11... | collective-permute-start | bytes 1572872 | tf_op jit(solution)/shard_map/ppermute | solution.py:338
  108.1 10.4 %collective-permute-start.4 = (f32[224,512]{1,0:T(8,128)S(1)}, f32[224,512]{1,0:T(8,128)S(1)}, u32[]{:S(2)}, u32[]{:S(2)}) collective-permute-start(f32[224,512]{1,0:T(8,128)S(1)} %get-tuple-element.100), channel_id=1, source_target_pairs={{0,2},{2,4},{4,6},{6,8},{8,10},{10,12},{12,14},{14,16},{16,18},{18... | collective-permute-start | bytes 1376264 | tf_op jit(solution)/shard_map/ppermute | solution.py:334
  112.3 0.9 copy-start.5
  112.3 1.0 copy-start.7
  112.3 1.0 copy-start.9
  119.8 17.9 %copy-start.3 = (f32[3,31]{1,0:T(4,128)S(1)}, f32[3,31]{1,0:T(4,128)}, u32[]{:S(2)}) copy-start(f32[3,31]{1,0:T(4,128)} %spread_ref.5) | copy-start | bytes 1120
  119.8 13.2 %collective-permute-start.6 = (f32[256,512]{1,0:T(8,128)S(1)}, f32[256,512]{1,0:T(8,128)S(1)}, u32[]{:S(2)}, u32[]{:S(2)}) collective-permute-start(f32[256,512]{1,0:T(8,128)S(1)} %get-tuple-element.109.refs_2_), channel_id=1, source_target_pairs={{1,3},{3,5},{5,7},{7,9},{9,11},{11,13},{13,15},{15,17},{17,19},{19... | collective-permute-start | bytes 1572872 | tf_op jit(solution)/shard_map/ppermute | solution.py:332
  121.8 18.0 %collective-permute-start.8 = (f32[256,512]{1,0:T(8,128)S(1)}, f32[256,512]{1,0:T(8,128)S(1)}, u32[]{:S(2)}, u32[]{:S(2)}) collective-permute-start(f32[256,512]{1,0:T(8,128)S(1)} %get-tuple-element.109.refs_2_), channel_id=1, source_target_pairs={{0,1},{1,0},{2,3},{3,2},{4,5},{5,4},{6,7},{7,6},{8,9},{9,8},{10,11... | collective-permute-start | bytes 1572872 | tf_op jit(solution)/shard_map/ppermute | solution.py:333
  133.0 7.8 %collective-permute-start.7 = (f32[256,512]{1,0:T(8,128)S(1)}, f32[256,512]{1,0:T(8,128)S(1)}, u32[]{:S(2)}, u32[]{:S(2)}) collective-permute-start(f32[256,512]{1,0:T(8,128)S(1)} %collective-permute-done.6.refs_2_), channel_id=1, source_target_pairs={{0,1},{1,0},{2,3},{3,2},{4,5},{5,4},{6,7},{7,6},{8,9},{9,8},{10,11... | collective-permute-start | bytes 1572872 | tf_op jit(solution)/shard_map/ppermute | solution.py:338
  135.0 10.4 %collective-permute-start.9 = (f32[224,512]{1,0:T(8,128)S(1)}, f32[224,512]{1,0:T(8,128)S(1)}, u32[]{:S(2)}, u32[]{:S(2)}) collective-permute-start(f32[224,512]{1,0:T(8,128)S(1)} %get-tuple-element.116), channel_id=1, source_target_pairs={{0,2},{2,4},{4,6},{6,8},{8,10},{10,12},{12,14},{14,16},{16,18},{18... | collective-permute-start | bytes 1376264 | tf_op jit(solution)/shard_map/ppermute | solution.py:334
  146.7 13.2 %collective-permute-start.10 = (f32[256,512]{1,0:T(8,128)S(1)}, f32[256,512]{1,0:T(8,128)S(1)}, u32[]{:S(2)}, u32[]{:S(2)}) collective-permute-start(f32[256,512]{1,0:T(8,128)S(1)} %get-tuple-element.125.refs_2_), channel_id=1, source_target_pairs={{1,3},{3,5},{5,7},{7,9},{9,11},{11,13},{13,15},{15,17},{17,19},{19... | collective-permute-start | bytes 1572872 | tf_op jit(solution)/shard_map/ppermute | solution.py:332
  148.6 17.7 %collective-permute-start.12 = (f32[256,512]{1,0:T(8,128)S(1)}, f32[256,512]{1,0:T(8,128)S(1)}, u32[]{:S(2)}, u32[]{:S(2)}) collective-permute-start(f32[256,512]{1,0:T(8,128)S(1)} %get-tuple-element.125.refs_2_), channel_id=1, source_target_pairs={{0,1},{1,0},{2,3},{3,2},{4,5},{5,4},{6,7},{7,6},{8,9},{9,8},{10,11... | collective-permute-start | bytes 1572872 | tf_op jit(solution)/shard_map/ppermute | solution.py:333
  159.9 7.4 %collective-permute-start.11 = (f32[256,512]{1,0:T(8,128)S(1)}, f32[256,512]{1,0:T(8,128)S(1)}, u32[]{:S(2)}, u32[]{:S(2)}) collective-permute-start(f32[256,512]{1,0:T(8,128)S(1)} %collective-permute-done.10.refs_2_), channel_id=1, source_target_pairs={{0,1},{1,0},{2,3},{3,2},{4,5},{5,4},{6,7},{7,6},{8,9},{9,8},{10,11... | collective-permute-start | bytes 1572872 | tf_op jit(solution)/shard_map/ppermute | solution.py:338
  161.8 10.4 %collective-permute-start.13 = (f32[224,512]{1,0:T(8,128)S(1)}, f32[224,512]{1,0:T(8,128)S(1)}, u32[]{:S(2)}, u32[]{:S(2)}) collective-permute-start(f32[224,512]{1,0:T(8,128)S(1)} %get-tuple-element.132), channel_id=1, source_target_pairs={{0,2},{2,4},{4,6},{6,8},{8,10},{10,12},{12,14},{14,16},{16,18},{18... | collective-permute-start | bytes 1376264 | tf_op jit(solution)/shard_map/ppermute | solution.py:334
  173.5 13.2 %collective-permute-start.14 = (f32[256,512]{1,0:T(8,128)S(1)}, f32[256,512]{1,0:T(8,128)S(1)}, u32[]{:S(2)}, u32[]{:S(2)}) collective-permute-start(f32[256,512]{1,0:T(8,128)S(1)} %get-tuple-element.140.refs_2_), channel_id=1, source_target_pairs={{1,3},{3,5},{5,7},{7,9},{9,11},{11,13},{13,15},{15,17},{17,19},{19... | collective-permute-start | bytes 1572872 | tf_op jit(solution)/shard_map/ppermute | solution.py:332
  175.5 15.7 %collective-permute-start.16 = (f32[256,512]{1,0:T(8,128)S(1)}, f32[256,512]{1,0:T(8,128)S(1)}, u32[]{:S(2)}, u32[]{:S(2)}) collective-permute-start(f32[256,512]{1,0:T(8,128)S(1)} %get-tuple-element.140.refs_2_), channel_id=1, source_target_pairs={{0,1},{1,0},{2,3},{3,2},{4,5},{5,4},{6,7},{7,6},{8,9},{9,8},{10,11... | collective-permute-start | bytes 1572872 | tf_op jit(solution)/shard_map/ppermute | solution.py:333
  186.7 5.5 %collective-permute-start.15 = (f32[256,512]{1,0:T(8,128)S(1)}, f32[256,512]{1,0:T(8,128)S(1)}, u32[]{:S(2)}, u32[]{:S(2)}) collective-permute-start(f32[256,512]{1,0:T(8,128)S(1)} %collective-permute-done.14.refs_2_), channel_id=1, source_target_pairs={{0,1},{1,0},{2,3},{3,2},{4,5},{5,4},{6,7},{7,6},{8,9},{9,8},{10,11... | collective-permute-start | bytes 1572872 | tf_op jit(solution)/shard_map/ppermute | solution.py:338
  188.7 10.4 %collective-permute-start.17 = (f32[224,512]{1,0:T(8,128)S(1)}, f32[224,512]{1,0:T(8,128)S(1)}, u32[]{:S(2)}, u32[]{:S(2)}) collective-permute-start(f32[224,512]{1,0:T(8,128)S(1)} %get-tuple-element.147), channel_id=1, source_target_pairs={{0,2},{2,4},{4,6},{6,8},{8,10},{10,12},{12,14},{14,16},{16,18},{18... | collective-permute-start | bytes 1376264 | tf_op jit(solution)/shard_map/ppermute | solution.py:334
  199.5 4.5 %collective-permute-start.18 = (f32[128,512]{1,0:T(8,128)S(1)}, f32[128,512]{1,0:T(8,128)S(1)}, u32[]{:S(2)}, u32[]{:S(2)}) collective-permute-start(f32[128,512]{1,0:T(8,128)S(1)} %get-tuple-element.152), channel_id=1, source_target_pairs={{0,1},{1,0},{2,3},{3,2},{4,5},{5,4},{6,7},{7,6},{8,9},{9,8},{10,11... | collective-permute-start | bytes 786440 | tf_op jit(solution)/shard_map/ppermute | solution.py:352
